TPU v7x, 512 devices: a whole 4x8x8 slice. The times are simulated.
512 devices in a mesh: slab: 128 (over x, z, y_hi), blk: 4 (over y_lo, core).
Axes of the slice: x: 4, y: 8 (y_hi: 4, y_lo: 2; y = y_hi * 2 + y_lo), z: 8, core: 2. Of those that a mesh axis runs over, the one named last changes fastest.
Arguments:
- incident: float32 [256, 2, 336, 128], P('slab', None, 'blk'), may hold values from -6 to 6
- mie_coef: float32 [256, 2, 336], P('slab', None, 'blk'), may hold values from -0.6 to 0.6
- translation: bfloat16 [256, 8, 2, 336, 336], P('slab', None, None, 'blk'), may hold values from -0.078125 to 0.078125
- pair_shift: int32 [256, 8], P('slab'), may hold values from -1 to 1
- pair_member: int32 [256, 8], P('slab'), may hold values from 0 to 1
- positions: float32 [256, 3], P('slab'), may hold values from 0 to 1
- wave_index: int32 [256, 3], replicated, may hold values from -4 to 4
- plane_coef: bfloat16 [256, 2, 336], replicated, may hold values from -0.25 to 0.25
- ewald_weight: float32 [256], replicated, may hold values from 0.002 to 0.04
Outputs:
- basis_next: float32 [256, 2, 336, 128], P('slab', None, 'blk')
- residual: float32 [256, 2, 336, 128], P('slab', None, 'blk')
- hessenberg: float32 [9, 128], replicated
Inputs may be any that keep to these rules, and one draw needn't show every extreme that they name: `pair_shift`: each pair's source sphere lies in the target's slab or in one of the two slabs beside it on the periodic cycle of slabs.
All inputs are finite; a program needn't handle non-finite values.
Results may differ from a plain program's by a relative error of at most 0.004.
Values may be sent and summed in bfloat16 or wider, within the bound.
A program may use at most 64 MiB of HBM per device.

v0:
```python
import jax
import jax.numpy as jnp
from jax import lax
from jax.sharding import Mesh
from jax.sharding import PartitionSpec as P

SLAB = ("slab_0", "slab_1", "slab_2")
BLK = ("blk_0", "blk_1")
SLAB_BLK = ("slab_0", "slab_1", "slab_2", "blk_0", "blk_1")


two_pi = 6.283185307179586
epsilon = 1e-06
highest = lax.Precision.HIGHEST


def with_halo(cells, sides, width):
    for axis, dim in sides:
        count = lax.axis_size(axis)
        head = lax.slice_in_dim(cells, 0, width, axis=dim)
        tail = lax.slice_in_dim(cells, cells.shape[dim] - width, cells.shape[dim], axis=dim)
        cells = jnp.concatenate(
            [
                lax.ppermute(tail, axis, [(i, (i + 1) % count) for i in range(count)]),
                cells,
                lax.ppermute(head, axis, [((i + 1) % count, i) for i in range(count)]),
            ],
            axis=dim,
        )
    return cells


def joined_along(tiles, dim):
    tiles = jnp.moveaxis(tiles, 0, dim)
    shape = tiles.shape
    return tiles.reshape(*shape[:dim], shape[dim] * shape[dim + 1], *shape[dim + 2 :])


def copy_for_each(value, axis):
    length = lax.axis_size(axis)
    return lax.all_to_all(
        jnp.broadcast_to(value[None], (length, *value.shape)), axis, 0, 0, tiled=True
    )


def gather_directly(value, axis, dim):
    return joined_along(copy_for_each(value, axis), dim)


def over_axes(value, axes):
    for axis in axes:
        value = lax.psum(value, axis)
    return value


def complex_scale(coef_pair, basis):
    part_re = coef_pair[0] * basis[:, 0] - coef_pair[1] * basis[:, 1]
    part_im = coef_pair[0] * basis[:, 1] + coef_pair[1] * basis[:, 0]
    return jnp.stack([part_re, part_im], axis=1)


def inner_sum(left, right):
    part_re = jnp.sum(left[:, 0] * right[:, 0] + left[:, 1] * right[:, 1], axis=(0, 1))
    part_im = jnp.sum(left[:, 0] * right[:, 1] - left[:, 1] * right[:, 0], axis=(0, 1))
    return jnp.stack([part_re, part_im])


def plane_sums(projected, cos_part, sin_part):
    part_re = projected[:, 0, :, 0] - projected[:, 1, :, 1]
    part_im = projected[:, 0, :, 1] + projected[:, 1, :, 0]
    sum_re = jnp.sum(cos_part[:, :, None] * part_re + sin_part[:, :, None] * part_im, axis=1)
    sum_im = jnp.sum(cos_part[:, :, None] * part_im - sin_part[:, :, None] * part_re, axis=1)
    return jnp.stack([sum_re, sum_im], axis=1)


def plane_field(totals, coef_full, cos_part, sin_part, weights):
    total_re = totals[:, 0][:, None, :]
    total_im = totals[:, 1][:, None, :]
    turn_re = weights[:, None, None] * (
        cos_part[:, :, None] * total_re - sin_part[:, :, None] * total_im
    )
    turn_im = weights[:, None, None] * (
        cos_part[:, :, None] * total_im + sin_part[:, :, None] * total_re
    )
    turned = jnp.stack([turn_re, turn_im], axis=1)
    projected = jnp.einsum("gac,gbjn->jabcn", coef_full, turned, precision=highest)
    return jnp.stack(
        [projected[:, 0, 0] + projected[:, 1, 1], projected[:, 0, 1] - projected[:, 1, 0]], axis=1
    )


def apply_operator(
    vector, mie_coef, translation, source_rows, cos_part, sin_part, plane_coef, ewald_weight
):
    sphere_count = vector.shape[0]
    row_count = vector.shape[2]
    rounded = vector.astype(jnp.bfloat16)
    edge_field = with_halo(rounded, ((SLAB, 0),), sphere_count)
    extended = gather_directly(edge_field, BLK, 2)
    pair_count = translation.shape[0] * translation.shape[1]
    flat_trans = translation.reshape(pair_count, 2, row_count, translation.shape[4])
    sources = jnp.take(extended, source_rows, axis=0)
    product = jnp.einsum(
        "parc,pzcn->pazrn", flat_trans, sources, preferred_element_type=jnp.float32
    )
    near_re = product[:, 0, 0] - product[:, 1, 1]
    near_im = product[:, 0, 1] + product[:, 1, 0]
    near = (
        jnp.stack([near_re, near_im], axis=1)
        .reshape(sphere_count, translation.shape[1], 2, row_count, vector.shape[3])
        .sum(axis=1)
    )
    row_start = lax.axis_index(BLK) * row_count
    coef_rows = lax.dynamic_slice_in_dim(plane_coef, row_start, row_count, 2)
    projected = jnp.einsum(
        "gac,jbcn->gajbn", coef_rows, rounded, preferred_element_type=jnp.float32
    )
    totals = lax.psum(plane_sums(projected, cos_part, sin_part), SLAB_BLK)
    far = plane_field(totals, coef_rows.astype(jnp.float32), cos_part, sin_part, ewald_weight)
    summed = near + far
    scaled_re = (
        mie_coef[:, 0][:, :, None] * summed[:, 0] - mie_coef[:, 1][:, :, None] * summed[:, 1]
    )
    scaled_im = (
        mie_coef[:, 0][:, :, None] * summed[:, 1] + mie_coef[:, 1][:, :, None] * summed[:, 0]
    )
    return vector - jnp.stack([scaled_re, scaled_im], axis=1)


def squared(field):
    return jnp.sum(field * field, axis=(0, 1, 2))


def per_device(
    incident,
    mie_coef,
    translation,
    pair_shift,
    pair_member,
    positions,
    wave_index,
    plane_coef,
    ewald_weight,
):
    sphere_count = incident.shape[0]
    entries = sphere_count * lax.axis_size(SLAB) * incident.shape[2] * lax.axis_size(BLK)
    source_rows = ((pair_shift + 1) * sphere_count + pair_member).reshape(-1)
    angles = two_pi * jnp.sum(
        wave_index.astype(jnp.float32)[:, None, :] * positions[None, :, :], axis=-1
    )
    cos_part = jnp.cos(angles)
    sin_part = jnp.sin(angles)

    def operator(vector):
        return apply_operator(
            vector, mie_coef, translation, source_rows, cos_part, sin_part, plane_coef, ewald_weight
        )

    start_total = over_axes(squared(incident), SLAB_BLK)
    beta = jnp.sqrt(start_total / entries + epsilon)
    first = incident / beta
    image = operator(first)
    proj_sum = over_axes(inner_sum(first, image), SLAB_BLK)
    h_one_one = proj_sum / entries
    image = image - complex_scale(h_one_one, first)
    first_total = over_axes(squared(image), SLAB_BLK)
    h_two_one = jnp.sqrt(first_total / entries + epsilon)
    basis_next = image / h_two_one
    image = operator(basis_next)
    both_sums = (
        over_axes(inner_sum(first, image), SLAB_BLK),
        over_axes(inner_sum(basis_next, image), SLAB_BLK),
    )
    h_one_two = both_sums[0] / entries
    h_two_two = both_sums[1] / entries
    residual = image - complex_scale(h_one_two, first) - complex_scale(h_two_two, basis_next)
    last_total = over_axes(squared(residual), SLAB_BLK)
    h_three_two = jnp.sqrt(last_total / entries + epsilon)
    hessenberg = jnp.stack(
        [
            beta,
            h_one_one[0],
            h_one_one[1],
            h_two_one,
            h_one_two[0],
            h_one_two[1],
            h_two_two[0],
            h_two_two[1],
            h_three_two,
        ]
    )
    return (basis_next, residual, hessenberg)


def solution(mesh):
    torus = Mesh(
        mesh.devices.reshape(4, 8, 4, 2, 2), ("slab_0", "slab_1", "slab_2", "blk_0", "blk_1")
    )
    return jax.shard_map(
        per_device,
        mesh=torus,
        in_specs=(
            P(SLAB, None, BLK, None),
            P(SLAB, None, BLK),
            P(SLAB, None, None, BLK, None),
            P(SLAB, None),
            P(SLAB, None),
            P(SLAB, None),
            P(),
            P(),
            P(),
        ),
        out_specs=(P(SLAB, None, BLK, None), P(SLAB, None, BLK, None), P()),
        check_vma=False,
    )
```

profile of v0, /device:TPU:1, one launch (start us, length us, event | category | flops | bytes accessed | tf_op | source)
XLA Modules:
  0.0 842.6 jit_solution(11295606234036943234)
XLA Ops:
  7.3 1.2 multiply_reduce_fusion.2
  8.5 9.3 %psum.224 = f32[128]{0:T(128)S(1)} all-reduce(f32[128]{0:T(128)S(1)} %multiply_reduce_fusion.2), channel_id=1, replica_groups=mesh['slab_0'=4,'slab_1'=8,'slab_2'=4,'blk_0'=2,'blk_1'=2] {'slab_0'}, use_global_device_ids=true, to_apply=%region_1.0 | all-reduce | flops 128 | bytes 1024 | tf_op jit(solution)/shard_map/psum | solution.py:52
  17.8 19.5 %psum.225 = f32[128]{0:T(128)S(1)} all-reduce(f32[128]{0:T(128)S(1)} %psum.224), channel_id=1, replica_groups=mesh['slab_0'=4,'slab_1'=8,'slab_2'=4,'blk_0'=2,'blk_1'=2] {'slab_1'}, use_global_device_ids=true, to_apply=%region_2.0 | all-reduce | flops 128 | bytes 1024 | tf_op jit(solution)/shard_map/psum | solution.py:52
  37.2 10.9 %psum.226 = f32[128]{0:T(128)S(1)} all-reduce(f32[128]{0:T(128)S(1)} %psum.225), channel_id=1, replica_groups=mesh['slab_0'=4,'slab_1'=8,'slab_2'=4,'blk_0'=2,'blk_1'=2] {'slab_2'}, use_global_device_ids=true, to_apply=%region_3.0 | all-reduce | flops 128 | bytes 1024 | tf_op jit(solution)/shard_map/psum | solution.py:52
  48.1 4.1 psum.227
  52.2 11.4 %psum.228 = f32[128]{0:T(128)S(1)} all-reduce(f32[128]{0:T(128)S(1)} %psum.227), channel_id=1, replica_groups=mesh['slab_0'=4,'slab_1'=8,'slab_2'=4,'blk_0'=2,'blk_1'=2] {'blk_1'}, use_global_device_ids=true, to_apply=%region_5.0 | all-reduce | flops 128 | bytes 1024 | tf_op jit(solution)/shard_map/psum | solution.py:52
  64.1 0.9 copy_divide_fusion
  65.0 2.6 collective-permute-start
  67.6 9.1 %collective-permute-start.1 = (bf16[2,2,84,128]{3,2,0,1:T(8,128)(2,1)S(1)}, bf16[2,2,84,128]{3,2,0,1:T(8,128)(2,1)S(1)}, u32[]{:S(2)}, u32[]{:S(2)}) collective-permute-start(bf16[2,2,84,128]{3,2,0,1:T(8,128)(2,1)S(1)} %get-tuple-element.67), channel_id=1, source_target_pairs={{4,0},{8,4},{12,8},{16,12},{20,16},{24,20},{28,24},{32,28},{36,32}... | collective-permute-start | bytes 258056 | tf_op jit(solution)/shard_map/ppermute | solution.py:26
  76.7 0.7 convert_element_type.12
  77.3 0.8 copy.75
  78.3 1.2 fusion.41
  79.7 0.7 pad_maximum_fusion.2
  81.0 1.5 broadcast_in_dim.13
  82.5 4.3 all-to-all-start
  86.8 254.0 %all-reduce.8.cloned.1.call-done = f32[256,2,128]{2,0,1:T(8,128)} async-done(((f32[256,2,128]{2,0,1:T(8,128)}), f32[256,2,128]{2,0,1:T(8,128)}) %all-reduce.8.cloned.1.call-update) | async-done | bytes 262160 | tf_op jit(solution)/shard_map/psum | solution.py:118
  340.8 1.0 slice_bitcast_fusion.5
  342.1 1.3 convolution_bitcast_fusion.1
  343.4 1.1 copy.73
  344.5 1.3 reshape.274
  345.9 2.5 gather_fusion
  348.3 2.8 fusion.10
  352.2 8.1 psum.230
  360.2 12.0 %psum.231 = f32[2,128]{1,0:T(2,128)S(1)} all-reduce(f32[2,128]{1,0:T(2,128)S(1)} %psum.230), channel_id=1, replica_groups=mesh['slab_0'=4,'slab_1'=8,'slab_2'=4,'blk_0'=2,'blk_1'=2] {'slab_1'}, use_global_device_ids=true, to_apply=%region_14.16 | all-reduce | flops 256 | bytes 2048 | tf_op jit(solution)/shard_map/psum | solution.py:52
  372.2 9.2 %psum.232 = f32[2,128]{1,0:T(2,128)S(1)} all-reduce(f32[2,128]{1,0:T(2,128)S(1)} %psum.231), channel_id=1, replica_groups=mesh['slab_0'=4,'slab_1'=8,'slab_2'=4,'blk_0'=2,'blk_1'=2] {'slab_2'}, use_global_device_ids=true, to_apply=%region_15.17 | all-reduce | flops 256 | bytes 2048 | tf_op jit(solution)/shard_map/psum | solution.py:52
  381.4 5.3 psum.233
  386.7 9.9 %psum.234 = f32[2,128]{1,0:T(2,128)S(1)} all-reduce(f32[2,128]{1,0:T(2,128)S(1)} %psum.233), channel_id=1, replica_groups=mesh['slab_0'=4,'slab_1'=8,'slab_2'=4,'blk_0'=2,'blk_1'=2] {'blk_1'}, use_global_device_ids=true, to_apply=%region_17.19 | all-reduce | flops 256 | bytes 2048 | tf_op jit(solution)/shard_map/psum | solution.py:52
  397.3 6.1 psum.235
  403.4 11.3 %psum.236 = f32[128]{0:T(128)S(1)} all-reduce(f32[128]{0:T(128)S(1)} %psum.235), channel_id=1, replica_groups=mesh['slab_0'=4,'slab_1'=8,'slab_2'=4,'blk_0'=2,'blk_1'=2] {'slab_1'}, use_global_device_ids=true, to_apply=%region_20.22 | all-reduce | flops 128 | bytes 1024 | tf_op jit(solution)/shard_map/psum | solution.py:52
  414.7 9.5 %psum.237 = f32[128]{0:T(128)S(1)} all-reduce(f32[128]{0:T(128)S(1)} %psum.236), channel_id=1, replica_groups=mesh['slab_0'=4,'slab_1'=8,'slab_2'=4,'blk_0'=2,'blk_1'=2] {'slab_2'}, use_global_device_ids=true, to_apply=%region_21.23 | all-reduce | flops 128 | bytes 1024 | tf_op jit(solution)/shard_map/psum | solution.py:52
  424.2 3.8 psum.238
  427.9 10.7 %psum.239 = f32[128]{0:T(128)S(1)} all-reduce(f32[128]{0:T(128)S(1)} %psum.238), channel_id=1, replica_groups=mesh['slab_0'=4,'slab_1'=8,'slab_2'=4,'blk_0'=2,'blk_1'=2] {'blk_1'}, use_global_device_ids=true, to_apply=%region_23.25 | all-reduce | flops 128 | bytes 1024 | tf_op jit(solution)/shard_map/psum | solution.py:52
  439.2 0.7 fusion.62
  439.9 1.9 collective-permute-start.2
  441.8 9.7 %collective-permute-start.3 = (bf16[2,2,84,128]{3,2,0,1:T(8,128)(2,1)S(1)}, bf16[2,2,84,128]{3,2,0,1:T(8,128)(2,1)S(1)}, u32[]{:S(2)}, u32[]{:S(2)}) collective-permute-start(bf16[2,2,84,128]{3,2,0,1:T(8,128)(2,1)S(1)} %get-tuple-element.40), channel_id=1, source_target_pairs={{4,0},{8,4},{12,8},{16,12},{20,16},{24,20},{28,24},{32,28},{36,32}... | collective-permute-start | bytes 258056 | tf_op jit(solution)/shard_map/ppermute | solution.py:26
  451.5 1.4 collective-permute-done.2
  452.9 2.3 collective-permute-done.3
  455.5 1.5 broadcast_in_dim.14
  457.0 4.0 all-to-all-start.1
  461.0 1.2 fusion.37
  462.4 0.7 pad_maximum_fusion.3
  463.2 0.8 copy.90
  463.9 270.9 %all-reduce.10.cloned.1.call-done = f32[256,2,128]{2,0,1:T(8,128)} async-done(((f32[256,2,128]{2,0,1:T(8,128)}), f32[256,2,128]{2,0,1:T(8,128)}) %all-reduce.10.cloned.1.call-update) | async-done | bytes 262160 | tf_op jit(solution)/shard_map/psum | solution.py:118
  734.8 1.0 slice_bitcast_fusion.3
  735.8 0.9 subtract_multiply_fusion
  736.7 1.3 convolution_bitcast_fusion
  738.0 0.7 fusion.33
  738.7 1.1 copy.82
  739.8 1.3 reshape.277
  741.2 2.6 gather_fusion.1
  743.7 2.8 fusion.15
  746.8 0.6 copy-done.2
  747.7 8.1 all-reduce.2
  755.8 12.0 %all-reduce = (f32[2,128]{1,0:T(2,128)S(1)}, f32[2,128]{1,0:T(2,128)S(1)}) all-reduce(f32[2,128]{1,0:T(2,128)S(1)} %get-tuple-element.32, f32[2,128]{1,0:T(2,128)S(1)} %get-tuple-element.33), channel_id=1, replica_groups=mesh['slab_0'=4,'slab_1'=8,'slab_2'=4,'blk_0'=2,'blk_1'=2] {'slab_1'}, use_global_device_ids=true, to_apply=%region_31.33 | all-reduce | flops 512 | bytes 4096 | tf_op jit(solution)/shard_map/psum | solution.py:52
  767.8 9.2 %all-reduce.1 = (f32[2,128]{1,0:T(2,128)S(1)}, f32[2,128]{1,0:T(2,128)S(1)}) all-reduce(f32[2,128]{1,0:T(2,128)S(1)} %get-tuple-element.28, f32[2,128]{1,0:T(2,128)S(1)} %get-tuple-element.29), channel_id=1, replica_groups=mesh['slab_0'=4,'slab_1'=8,'slab_2'=4,'blk_0'=2,'blk_1'=2] {'slab_2'}, use_global_device_ids=true, to_apply=%region_32.34 | all-reduce | flops 512 | bytes 4096 | tf_op jit(solution)/shard_map/psum | solution.py:52
  777.0 5.3 all-reduce.4
  782.2 9.9 %all-reduce.3 = (f32[2,128]{1,0:T(2,128)S(1)}, f32[2,128]{1,0:T(2,128)S(1)}) all-reduce(f32[2,128]{1,0:T(2,128)S(1)} %get-tuple-element.36, f32[2,128]{1,0:T(2,128)S(1)} %get-tuple-element.37), channel_id=1, replica_groups=mesh['slab_0'=4,'slab_1'=8,'slab_2'=4,'blk_0'=2,'blk_1'=2] {'blk_1'}, use_global_device_ids=true, to_apply=%region_34.36 | all-reduce | flops 512 | bytes 4096 | tf_op jit(solution)/shard_map/psum | solution.py:52
  792.3 6.1 psum.251
  798.4 11.3 %psum.252 = f32[128]{0:T(128)S(1)} all-reduce(f32[128]{0:T(128)S(1)} %psum.251), channel_id=1, replica_groups=mesh['slab_0'=4,'slab_1'=8,'slab_2'=4,'blk_0'=2,'blk_1'=2] {'slab_1'}, use_global_device_ids=true, to_apply=%region_44.46 | all-reduce | flops 128 | bytes 1024 | tf_op jit(solution)/shard_map/psum | solution.py:52
  809.7 9.5 %psum.253 = f32[128]{0:T(128)S(1)} all-reduce(f32[128]{0:T(128)S(1)} %psum.252), channel_id=1, replica_groups=mesh['slab_0'=4,'slab_1'=8,'slab_2'=4,'blk_0'=2,'blk_1'=2] {'slab_2'}, use_global_device_ids=true, to_apply=%region_45.47 | all-reduce | flops 128 | bytes 1024 | tf_op jit(solution)/shard_map/psum | solution.py:52
  819.2 3.8 psum.254
  823.0 10.7 %psum.255 = f32[128]{0:T(128)S(1)} all-reduce(f32[128]{0:T(128)S(1)} %psum.254), channel_id=1, replica_groups=mesh['slab_0'=4,'slab_1'=8,'slab_2'=4,'blk_0'=2,'blk_1'=2] {'blk_1'}, use_global_device_ids=true, to_apply=%region_47.49 | all-reduce | flops 128 | bytes 1024 | tf_op jit(solution)/shard_map/psum | solution.py:52
  833.7 0.8 copy.91
  834.5 1.2 stack.142
  (90 shorter events, 5.0 us)
Async XLA Ops:
  7.2 341.2 %copy-start = (bf16[2,8,2,84,336]{4,2,3,1,0:T(2,128)(2,1)S(1)}, bf16[2,8,2,84,336]{4,2,3,1,0:T(2,128)(2,1)}, u32[]{:S(2)}) copy-start(bf16[2,8,2,84,336]{4,2,3,1,0:T(2,128)(2,1)} %param.13) | copy-start | bytes 5419012
  7.2 73.3 %copy-start.12 = (f32[2,2,84]{2,1,0:T(2,128)S(1)}, f32[2,2,84]{2,1,0:T(2,128)}, u32[]{:S(2)}) copy-start(f32[2,2,84]{2,1,0:T(2,128)} %param.12) | copy-start | bytes 4036
  7.2 73.3 %copy-start.14 = (s32[2,8]{1,0:T(2,128)S(1)}, s32[2,8]{1,0:T(2,128)}, u32[]{:S(2)}) copy-start(s32[2,8]{1,0:T(2,128)} %param.14) | copy-start | bytes 196
  7.2 73.3 %copy-start.13 = (s32[2,8]{1,0:T(2,128)S(1)}, s32[2,8]{1,0:T(2,128)}, u32[]{:S(2)}) copy-start(s32[2,8]{1,0:T(2,128)} %param.15) | copy-start | bytes 196
  7.2 333.6 %all-reduce.8.cloned.1.call-start = ((), (), s32[]{:S(2)}) async-start(), calls=%async_computation.2 | async-start | bytes 524288 | tf_op jit(solution)/shard_map/psum | solution.py:118
  64.1 333.1 %copy-start.9 = (f32[128]{0:T(128)}, f32[128]{0:T(128)S(1)}, u32[]{:S(2)}) copy-start(f32[128]{0:T(128)S(1)} %get-tuple-element.81) | copy-start | bytes 1540
  65.0 15.6 %collective-permute-start = (bf16[2,2,84,128]{3,2,0,1:T(8,128)(2,1)S(1)}, bf16[2,2,84,128]{3,2,0,1:T(8,128)(2,1)S(1)}, u32[]{:S(2)}, u32[]{:S(2)}) collective-permute-start(bf16[2,2,84,128]{3,2,0,1:T(8,128)(2,1)S(1)} %get-tuple-element.67), channel_id=1, source_target_pairs={{0,4},{4,8},{8,12},{12,16},{16,20},{20,24},{24,28},{28,32},{32,36}... | collective-permute-start | bytes 258056 | tf_op jit(solution)/shard_map/ppermute | solution.py:24
  67.6 13.2 %collective-permute-start.1 = (bf16[2,2,84,128]{3,2,0,1:T(8,128)(2,1)S(1)}, bf16[2,2,84,128]{3,2,0,1:T(8,128)(2,1)S(1)}, u32[]{:S(2)}, u32[]{:S(2)}) collective-permute-start(bf16[2,2,84,128]{3,2,0,1:T(8,128)(2,1)S(1)} %get-tuple-element.67), channel_id=1, source_target_pairs={{4,0},{8,4},{12,8},{16,12},{20,16},{24,20},{28,24},{32,28},{36,32}... | collective-permute-start | bytes 258056 | tf_op jit(solution)/shard_map/ppermute | solution.py:26
  79.7 262.1 %copy-start.11 = (f32[256]{0:T(256)S(1)}, f32[256]{0:T(256)}, u32[]{:S(2)}) copy-start(f32[256]{0:T(256)} %param.19) | copy-start | bytes 3076
  80.5 270.9 %copy-start.3 = (f32[2,1,84]{2,1,0:T(1,128)}, f32[2,1,84]{2,1,0:T(1,128)S(1)}, u32[]{:S(2)}) copy-start(f32[2,1,84]{2,1,0:T(1,128)S(1)} %get-tuple-element.68) | copy-start | bytes 2020
  80.5 270.9 %copy-start.5 = (f32[2,1,84]{2,1,0:T(1,128)}, f32[2,1,84]{2,1,0:T(1,128)S(1)}, u32[]{:S(2)}) copy-start(f32[2,1,84]{2,1,0:T(1,128)S(1)} %get-tuple-element.69) | copy-start | bytes 2020
  82.5 260.8 %all-to-all-start = ((bf16[4,6,2,84,128]{4,2,3,1,0:T(2,128)(2,1)}), bf16[4,6,2,84,128]{4,2,3,1,0:T(2,128)(2,1)S(1)}, u32[]{:S(2)}, u32[]{:S(2)}) async-start(bf16[4,6,2,84,128]{4,2,3,1,0:T(2,128)(2,1)} %broadcast_in_dim.13), calls=%async_computation | async-start | bytes 2064384 | tf_op jit(solution)/shard_map/all_to_all | solution.py:41
  86.8 261.5 %copy-start.17 = (pred[16]{0:T(512)(128)(4,1)}, pred[16]{0:T(512)(128)(4,1)S(1)}, u32[]{:S(2)}) copy-start(pred[16]{0:T(512)(128)(4,1)S(1)} %compare_and_fusion) | copy-start | bytes 52
  86.8 259.0 %copy-start.10 = (s32[1024]{0:T(1024)}, s32[1024]{0:T(1024)S(1)}, u32[]{:S(2)}) copy-start(s32[1024]{0:T(1024)S(1)} %pad_clamp_fusion) | copy-start | bytes 12292
  351.1 0.9 copy-start.1
  396.6 0.6 copy-start.7
  439.9 13.0 %collective-permute-start.2 = (bf16[2,2,84,128]{3,2,0,1:T(8,128)(2,1)S(1)}, bf16[2,2,84,128]{3,2,0,1:T(8,128)(2,1)S(1)}, u32[]{:S(2)}, u32[]{:S(2)}) collective-permute-start(bf16[2,2,84,128]{3,2,0,1:T(8,128)(2,1)S(1)} %get-tuple-element.40), channel_id=1, source_target_pairs={{0,4},{4,8},{8,12},{12,16},{16,20},{20,24},{24,28},{28,32},{32,36}... | collective-permute-start | bytes 258056 | tf_op jit(solution)/shard_map/ppermute | solution.py:24
  441.8 13.4 %collective-permute-start.3 = (bf16[2,2,84,128]{3,2,0,1:T(8,128)(2,1)S(1)}, bf16[2,2,84,128]{3,2,0,1:T(8,128)(2,1)S(1)}, u32[]{:S(2)}, u32[]{:S(2)}) collective-permute-start(bf16[2,2,84,128]{3,2,0,1:T(8,128)(2,1)S(1)} %get-tuple-element.40), channel_id=1, source_target_pairs={{4,0},{8,4},{12,8},{16,12},{20,16},{24,20},{28,24},{32,28},{36,32}... | collective-permute-start | bytes 258056 | tf_op jit(solution)/shard_map/ppermute | solution.py:26
  457.0 281.7 %all-to-all-start.1 = ((bf16[4,6,2,84,128]{4,2,3,1,0:T(2,128)(2,1)}), bf16[4,6,2,84,128]{4,2,3,1,0:T(2,128)(2,1)S(1)}, u32[]{:S(2)}, u32[]{:S(2)}) async-start(bf16[4,6,2,84,128]{4,2,3,1,0:T(2,128)(2,1)} %broadcast_in_dim.14), calls=%async_computation.1 | async-start | bytes 2064384 | tf_op jit(solution)/shard_map/all_to_all | solution.py:41
  461.0 273.8 %all-reduce.10.cloned.1.call-start = ((), (), s32[]{:S(2)}) async-start(), calls=%async_computation.3 | async-start | bytes 524288 | tf_op jit(solution)/shard_map/psum | solution.py:118
  741.1 2.6 copy-start.18
  746.5 0.9 copy-start.2
  746.6 0.9 copy-start.4
  746.6 0.9 copy-start.6
  746.7 87.8 %copy-start.8 = (f32[2,128]{1,0:T(2,128)S(1)}, f32[2,128]{1,0:T(2,128)}, u32[]{:S(2)}) copy-start(f32[2,128]{1,0:T(2,128)} %copy-done.7) | copy-start | bytes 3076
  746.7 87.8 %copy-start.15 = (f32[1,128]{1,0:T(1,128)S(1)}, f32[1,128]{1,0:T(1,128)}, u32[]{:S(2)}) copy-start(f32[1,128]{1,0:T(1,128)} %get-tuple-element.80) | copy-start | bytes 1540
  746.7 87.8 %copy-start.16 = (f32[1,128]{1,0:T(1,128)S(1)}, f32[1,128]{1,0:T(1,128)}, u32[]{:S(2)}) copy-start(f32[1,128]{1,0:T(1,128)} %get-tuple-element.78) | copy-start | bytes 1540
Sparse Core Ops, SparseCore 0:
  80.6 260.1 all-reduce.7
  466.8 268.0 all-reduce.9
where the time goes:
time: 844 us; the launch traced here: 843 us
  waiting for transfers between devices  529 us (63%)
  blocking collectives  227 us (27%)
  starting transfers between devices  31.5 us (4%)
  local copies, waits for them, and re-layouts  20.8 us (2%)
  between operations  14.6 us (2%)
  matrix products  10.6 us (1%)
  other arithmetic  9.76 us (1%)
    psum x2, waiting for transfers between devices, apply_operator(): totals = lax.psum(plane_sums(projected, cos_part, sin_part), SLAB_BLK)  525 us
    psum x25, blocking collectives, over_axes(): value = lax.psum(value, axis)  227 us
    ppermute x2, starting transfers between devices, with_halo(): lax.ppermute(head, axis, [((i + 1) % count, i) for i in range(count)])  18.7 us
  transfers between devices with their start and end apart: 8, of which 5 were waited for; matrix products, arithmetic and copies ran while one was open for 2% of the time, Pallas kernels for 0%

commit v1 on v0

v1 whole, which is shorter than its diff:
```python
import functools

import jax
import jax.numpy as jnp
from jax import lax
from jax.experimental import pallas as pl
from jax.experimental.pallas import tpu as pltpu
from jax.sharding import PartitionSpec as P

MESH = pl.DeviceIdType.MESH
SLAB = "slab"
BLK = "blk"
two_pi = 6.283185307179586
epsilon = 1e-06

ROWS = 16


def pair_swap(field, even):
    count = field.shape[0]
    return jnp.where(even, pltpu.roll(field, count - 1, 0), pltpu.roll(field, 1, 0))


def complex_rows(coef_re, coef_im, field, swapped, even):
    return coef_re * field + jnp.where(even, -coef_im, coef_im) * swapped


def inner_rows(left, right, right_swapped, even):
    real = jnp.sum(left * right, axis=0, keepdims=True)
    cross = left * right_swapped
    imag = jnp.sum(jnp.where(even, cross, -cross), axis=0, keepdims=True)
    return real, imag


def kernel(
    quads,
    highs,
    spheres,
    pairs,
    coefs,
    entries,
    source_ref,
    start_ref,
    gather_ref,
    spread_ref,
    trig_ref,
    mie_ref,
    trans_ref,
    next_ref,
    residual_ref,
    hess_ref,
    piece_ref,
    halo_ref,
    stage_ref,
    join_ref,
    joined_ref,
    cut_ref,
    part_ref,
    line_ref,
    sums_ref,
    gram_ref,
    near_ref,
    send_sem,
    recv_sem,
    halo_sem,
):
    blocks = 4
    slabs = quads * highs
    line_size = highs * blocks
    slab = lax.axis_index(SLAB)
    blk = lax.axis_index(BLK)
    quad = slab // highs
    high = slab % highs
    core = blk % 2
    low = blk // 2
    spot = high * blocks + blk
    rows = coefs // blocks
    wide = 2 * rows
    total = spheres * wide
    waves = gather_ref.shape[0] // 2

    def plane_peer(step):
        return (lax.rem(quad + step, quads) * highs + high, blk)

    def line_peer(step):
        other = lax.rem(spot + step, line_size)
        return (quad * highs + other // blocks, lax.rem(other, blocks))

    def shifted(step):
        return lax.rem(slab + step + slabs, slabs)

    barrier = pltpu.get_barrier_semaphore()

    @pl.loop(1, quads)
    def _(step):
        pl.semaphore_signal(barrier, inc=1, device_id=plane_peer(step), device_id_type=MESH)

    @pl.loop(1, line_size)
    def _(step):
        pl.semaphore_signal(barrier, inc=1, device_id=line_peer(step), device_id_type=MESH)

    for step in (-1, 1):
        for side in (0, 1):
            pl.semaphore_signal(
                barrier, inc=1, device_id=(shifted(step), side * 2 + core), device_id_type=MESH
            )
    greeted = quads - 1 + line_size - 1 + 4

    even = (lax.broadcasted_iota(jnp.int32, (wide, 128), 0) % 2) == 0

    def make_piece(turn, source):
        for sphere in range(spheres):
            for part in range(2):
                stage_ref[0, pl.ds((2 * sphere + part) * rows, rows), :] = source[
                    pl.ds(sphere * wide + part, rows, stride=2), :
                ]
        piece_ref[turn] = stage_ref[0].astype(jnp.bfloat16)

    def send(src, dst, sems, slot, device):
        return pltpu.make_async_remote_copy(
            src_ref=src,
            dst_ref=dst,
            send_sem=send_sem.at[slot],
            recv_sem=sems,
            device_id=device,
            device_id_type=MESH,
        )

    def halo_copies(turn):
        own = piece_ref.at[turn]
        out = []
        slot = 24 + 11 * turn
        for step, side in ((1, 0), (1, 1), (-1, 0), (-1, 1)):
            out.append(
                send(
                    own,
                    halo_ref.at[turn, 1 - step, blk],
                    halo_sem.at[turn, 1 - step, blk],
                    slot + len(out),
                    (shifted(step), side * 2 + core),
                )
            )
        for device in ((slab, (1 - low) * 2 + core), (slab, low * 2 + 1 - core)):
            out.append(
                send(
                    own,
                    halo_ref.at[turn, 1, blk],
                    halo_sem.at[turn, 1, blk],
                    slot + len(out),
                    device,
                )
            )
        return out

    def forward_copies(turn):
        out = []
        slot = 30 + 11 * turn
        for place, side in ((1, 1 - low), (0, 0), (0, 1), (2, 0), (2, 1)):
            index = side * 2 + core
            out.append(
                send(
                    halo_ref.at[turn, place, index],
                    halo_ref.at[turn, place, index],
                    halo_sem.at[turn, place, index],
                    slot + len(out),
                    (slab, low * 2 + 1 - core),
                )
            )
        return out

    def exchange(src_of, dst, turn_slot, peer, size):
        @pl.loop(1, size)
        def _(step):
            send(src_of(step), dst, recv_sem.at[turn_slot], turn_slot, peer(step)).start()

    def drain(block, turn_slot, size, what):
        ref = block.at[pl.ds(0, size - 1)]
        copy = send(ref, ref, recv_sem.at[turn_slot], turn_slot, (slab, blk))
        if what == "recv":
            copy.wait_recv()
        else:
            copy.wait_send()

    def project(field):
        rounded = jnp.concatenate(
            [
                field[sphere * wide : (sphere + 1) * wide].astype(jnp.bfloat16)
                for sphere in range(spheres)
            ],
            axis=1,
        )
        product = jnp.dot(gather_ref[...], rounded, preferred_element_type=jnp.float32)
        sum_re = jnp.zeros((waves, 128), jnp.float32)
        sum_im = jnp.zeros((waves, 128), jnp.float32)
        for sphere in range(spheres):
            lanes = slice(128 * sphere, 128 * (sphere + 1))
            part_re = product[:waves, lanes]
            part_im = product[waves:, lanes]
            cos_part = trig_ref[:, sphere : sphere + 1]
            sin_part = trig_ref[:, spheres + sphere : spheres + sphere + 1]
            sum_re = sum_re + cos_part * part_re + sin_part * part_im
            sum_im = sum_im + cos_part * part_im - sin_part * part_re
        return sum_re, sum_im

    def cut(turn, sums):
        shards = waves // ROWS
        for part in range(2):
            cut_ref[turn, pl.ds(part * shards, shards)] = (
                sums[part].astype(jnp.bfloat16).reshape(shards, ROWS, 128)
            )

    shard_count = 2 * waves // ROWS
    per_device = shard_count // quads

    def shards_of(ref, turn, owner):
        return ref.at[turn, pl.ds(owner * per_device, per_device)]

    def start_scatter(turn):
        exchange(
            lambda step: shards_of(cut_ref, turn, lax.rem(quad + step, quads)),
            part_ref.at[turn, quad],
            10 * turn + 2,
            plane_peer,
            quads,
        )

    def finish_scatter(turn):
        part_ref[turn, quad] = cut_ref[turn, pl.ds(quad * per_device, per_device)]
        drain(part_ref.at[turn], 10 * turn + 2, quads, "recv")
        value = part_ref[turn].astype(jnp.float32).sum(axis=0)
        line_ref[turn, spot] = value.astype(jnp.bfloat16)

    def start_line(turn):
        exchange(
            lambda step: line_ref.at[turn, spot],
            line_ref.at[turn, spot],
            10 * turn + 3,
            line_peer,
            line_size,
        )

    def finish_line(turn):
        drain(line_ref.at[turn], 10 * turn + 3, line_size, "recv")
        value = line_ref[turn].astype(jnp.float32).sum(axis=0)
        sums_ref[turn, pl.ds(quad * per_device, per_device)] = value.astype(jnp.bfloat16)

    def start_gather(turn):
        exchange(
            lambda step: shards_of(sums_ref, turn, quad),
            shards_of(sums_ref, turn, quad),
            10 * turn + 4,
            plane_peer,
            quads,
        )

    def finish_gather(turn):
        ref = sums_ref.at[turn, pl.ds(0, (quads - 1) * per_device)]
        send(ref, ref, recv_sem.at[10 * turn + 4], 10 * turn + 4, (slab, blk)).wait_recv()

    def far_field(turn):
        shards = waves // ROWS
        sum_re = sums_ref[turn, pl.ds(0, shards)].astype(jnp.float32).reshape(waves, 128)
        sum_im = sums_ref[turn, pl.ds(shards, shards)].astype(jnp.float32).reshape(waves, 128)
        weight = trig_ref[:, 2 * spheres : 2 * spheres + 1]
        turned_re, turned_im = [], []
        for sphere in range(spheres):
            cos_part = weight * trig_ref[:, sphere : sphere + 1]
            sin_part = weight * trig_ref[:, spheres + sphere : spheres + sphere + 1]
            turned_re.append((cos_part * sum_re - sin_part * sum_im).astype(jnp.bfloat16))
            turned_im.append((cos_part * sum_im + sin_part * sum_re).astype(jnp.bfloat16))
        turned = jnp.concatenate(
            [jnp.concatenate(turned_re, axis=1), jnp.concatenate(turned_im, axis=1)], axis=0
        )
        return jnp.dot(spread_ref[...], turned, preferred_element_type=jnp.float32)

    def join(turn, place):
        for index in range(blocks):
            stage_ref[index] = halo_ref[turn, place, index].astype(jnp.float32)
        for sphere in range(spheres):
            for part in range(2):
                for index in range(blocks):
                    join_ref[
                        pl.ds(index * rows, rows), pl.ds(128 * part, 128)
                    ] = stage_ref[index, pl.ds((2 * sphere + part) * rows, rows), :]
            joined_ref[place * spheres + sphere] = join_ref[...].astype(jnp.bfloat16)

    def near_field(sphere):
        total_product = jnp.zeros((wide, 256), jnp.float32)
        for pair in range(pairs):
            number = sphere * pairs + pair
            total_product = total_product + jnp.dot(
                trans_ref[number],
                joined_ref[source_ref[number]],
                preferred_element_type=jnp.float32,
            )
        swapped = pair_swap(total_product[:, 128:], even)
        near_ref[pl.ds(sphere * wide, wide), :] = total_product[:, :128] + jnp.where(
            even, -swapped, swapped
        )

    def operator(turn, source, sums):
        cut(turn, sums)
        start_scatter(turn)
        halo = halo_copies(turn)
        for copy in halo:
            copy.start()
        halo_ref[turn, 1, blk] = piece_ref[turn]
        finish_scatter(turn)
        start_line(turn)
        forward = forward_copies(turn)
        for copy in forward:
            copy.wait_recv()
            copy.start()
        other = 1 - core

        def arrived(place, side):
            index = side * 2 + other
            send(
                halo_ref.at[turn, place, index],
                halo_ref.at[turn, place, index],
                halo_sem.at[turn, place, index],
                10 * turn + 1,
                (slab, blk),
            ).wait_recv()

        finish_line(turn)
        start_gather(turn)
        for place in (1, 0, 2):
            for side in (0, 1):
                arrived(place, side)
            join(turn, place)
        for sphere in range(spheres):
            near_field(sphere)
        finish_gather(turn)
        far = far_field(turn)
        out = []
        for sphere in range(spheres):
            span = slice(sphere * wide, (sphere + 1) * wide)
            summed = near_ref[span] + far[:, 128 * sphere : 128 * (sphere + 1)]
            swapped = pair_swap(summed, even)
            out.append(mie_ref[span, 0:1] * summed + mie_ref[span, 1:2] * swapped)
        return out, halo, forward

    start = [start_ref[sphere * wide : (sphere + 1) * wide] for sphere in range(spheres)]
    make_piece(0, start_ref)
    first_sums = project(start_ref[...])
    pl.semaphore_wait(barrier, greeted)
    image, halo_one, forward_one = operator(0, start_ref, first_sums)

    def put_gram(slot, pairs_of):
        lines = []
        for name, left, right in pairs_of:
            real, imag = 0.0, 0.0
            for sphere in range(spheres):
                swapped = pair_swap(right[sphere], even)
                part_re, part_im = inner_rows(left[sphere], right[sphere], swapped, even)
                real, imag = real + part_re, imag + part_im
            lines.append(real)
            if name == "complex":
                lines.append(imag)
        lines.append(jnp.zeros((8 - len(lines), 128), jnp.float32))
        gram_ref[slot, spot] = jnp.concatenate(lines, axis=0)

    def start_gram(slot, turn_slot):
        exchange(
            lambda step: gram_ref.at[slot, spot],
            gram_ref.at[slot, spot],
            turn_slot,
            line_peer,
            line_size,
        )

    def turn_gram(slot, turn_slot):
        ref = gram_ref.at[slot, pl.ds(0, line_size - 1)]
        send(ref, ref, recv_sem.at[turn_slot], turn_slot, (slab, blk)).wait_recv()
        gram_ref[slot + 1, quad] = gram_ref[slot, pl.ds(0, line_size)].sum(axis=0)
        exchange(
            lambda step: gram_ref.at[slot + 1, quad],
            gram_ref.at[slot + 1, quad],
            turn_slot + 1,
            plane_peer,
            quads,
        )

    def end_gram(slot, turn_slot):
        ref = gram_ref.at[slot + 1, pl.ds(0, quads - 1)]
        send(ref, ref, recv_sem.at[turn_slot + 1], turn_slot + 1, (slab, blk)).wait_recv()
        return gram_ref[slot + 1, pl.ds(0, quads)].sum(axis=0)

    for sphere in range(spheres):
        next_ref[pl.ds(sphere * wide, wide), :] = image[sphere]
    make_piece(1, next_ref)
    second_sums = project(next_ref[...])
    put_gram(0, (("real", start, start), ("complex", start, image), ("real", image, image)))
    start_gram(0, 20)
    second, halo_two, forward_two = operator(1, next_ref, second_sums)
    put_gram(2, (("complex", start, second), ("complex", image, second), ("real", second, second)))
    start_gram(2, 22)
    turn_gram(0, 20)
    turn_gram(2, 22)
    early = end_gram(0, 20)
    late = end_gram(2, 22)

    norm_start = early[0:1]
    c_re, c_im = early[1:2], early[2:3]
    norm_image = early[3:4]
    d_re, d_im = late[0:1], late[1:2]
    e_re, e_im = late[2:3], late[3:4]
    norm_second = late[4:5]
    shift = entries * epsilon
    whole = norm_start + shift
    beta = jnp.sqrt(whole / entries)
    h11_re, h11_im = (norm_start - c_re) / whole, -c_im / whole
    g_re, g_im = (shift + c_re) / whole, c_im / whole
    apart = norm_image - (
        2.0 * (g_re * c_re + g_im * c_im) - (g_re * g_re + g_im * g_im) * norm_start
    )
    h21 = jnp.sqrt(jnp.maximum(apart, 0.0) / whole + epsilon)
    scale = 1.0 / (beta * h21)
    a_re, a_im = g_re * scale, g_im * scale
    both = shift / whole * scale / beta
    q_re, q_im = both * (norm_start - c_re), -both * c_im
    over = scale / beta
    gc_re, gc_im = g_re * c_re - g_im * c_im, g_re * c_im + g_im * c_re
    h12_re = (q_re + over * (d_re - gc_re)) / entries
    h12_im = (q_im + over * (d_im - gc_im)) / entries
    u_re = a_re * c_re + a_im * c_im - scale * norm_image
    u_im = a_re * c_im - a_im * c_re
    v_re = a_re * d_re + a_im * d_im - scale * e_re
    v_im = a_re * d_im - a_im * d_re - scale * e_im
    k_re = a_re * u_re - a_im * u_im - scale * v_re + h12_re * q_re + h12_im * q_im
    k_im = a_re * u_im + a_im * u_re - scale * v_im + h12_im * q_re - h12_re * q_im
    kap_re = epsilon / (h21 * h21) + k_re / entries
    kap_im = k_im / entries
    h22_re, h22_im = 1.0 - kap_re, -kap_im
    x_re = a_re * kap_re - a_im * kap_im - h12_re / beta
    x_im = a_re * kap_im + a_im * kap_re - h12_im / beta
    y_re = -scale * kap_re - a_re
    y_im = -scale * kap_im - a_im
    xy_re, xy_im = x_re * y_re + x_im * y_im, x_re * y_im - x_im * y_re
    left = (
        (x_re * x_re + x_im * x_im) * norm_start
        + (y_re * y_re + y_im * y_im) * norm_image
        + scale * scale * norm_second
        + 2.0 * (xy_re * c_re - xy_im * c_im)
        + 2.0 * scale * (x_re * d_re + x_im * d_im)
        + 2.0 * scale * (y_re * e_re + y_im * e_im)
    )
    h32 = jnp.sqrt(jnp.maximum(left, 0.0) / entries + epsilon)
    hess_ref[...] = jnp.concatenate(
        [
            beta,
            h11_re,
            h11_im,
            h21,
            h12_re,
            h12_im,
            h22_re,
            h22_im,
            h32,
            jnp.zeros((7, 128), jnp.float32),
        ],
        axis=0,
    )
    for sphere in range(spheres):
        span = pl.ds(sphere * wide, wide)
        one = start_ref[span, :]
        two = next_ref[span, :]
        one_swapped, two_swapped = pair_swap(one, even), pair_swap(two, even)
        residual_ref[span, :] = (
            complex_rows(x_re, x_im, one, one_swapped, even)
            + complex_rows(y_re, y_im, two, two_swapped, even)
            + scale * second[sphere]
        )
        next_ref[span, :] = complex_rows(a_re, a_im, one, one_swapped, even) - scale * two

    for copy in halo_one + forward_one + halo_two + forward_two:
        copy.wait_send()
    for turn in range(2):
        for slot, size, block in (
            (2, quads, part_ref.at[turn]),
            (3, line_size, line_ref.at[turn]),
            (4, quads, part_ref.at[turn]),
        ):
            drain(block, 10 * turn + slot, size, "send")
    for slot in (0, 2):
        drain(gram_ref.at[slot], 20 + slot, line_size, "send")
        drain(gram_ref.at[slot + 1], 21 + slot, quads, "send")


def per_device(
    quads,
    highs,
    incident,
    mie_coef,
    translation,
    pair_shift,
    pair_member,
    positions,
    wave_index,
    plane_coef,
    ewald_weight,
):
    spheres, _, rows, fields = incident.shape
    pairs = translation.shape[1]
    coefs = translation.shape[4]
    waves = plane_coef.shape[0]
    total = spheres * 2 * rows
    entries = quads * highs * spheres * coefs
    blocks = coefs // rows
    line_size = highs * blocks
    start = incident.transpose(0, 2, 1, 3).reshape(total, fields)
    trans = translation.transpose(0, 1, 3, 2, 4).reshape(spheres * pairs, 2 * rows, coefs)
    sources = ((pair_shift + 1) * spheres + pair_member).reshape(-1)
    angles = two_pi * jnp.sum(
        wave_index.astype(jnp.float32)[:, None, :] * positions[None, :, :], axis=-1
    )
    trig = jnp.concatenate([jnp.cos(angles), jnp.sin(angles), ewald_weight[:, None]], axis=1)
    mie_re = jnp.repeat(mie_coef[:, 0].reshape(-1), 2)
    mie_im = jnp.stack([-mie_coef[:, 1], mie_coef[:, 1]], axis=-1).reshape(-1)
    mie = jnp.stack([mie_re, mie_im], axis=1)
    coef_rows = lax.dynamic_slice_in_dim(plane_coef, lax.axis_index(BLK) * rows, rows, 2)
    coef_re, coef_im = coef_rows[:, 0].T, coef_rows[:, 1].T
    spread = jnp.stack(
        [
            jnp.concatenate([coef_re, coef_im], axis=1),
            jnp.concatenate([-coef_im, coef_re], axis=1),
        ],
        axis=1,
    ).reshape(2 * rows, 2 * waves)
    gather = spread.T
    shard_count = 2 * waves // ROWS
    per_quad = shard_count // quads
    vmem = pl.BlockSpec(memory_space=pltpu.VMEM)
    basis, residual, hess = pl.pallas_call(
        functools.partial(kernel, quads, highs, spheres, pairs, coefs, entries),
        out_shape=(
            jax.ShapeDtypeStruct((total, fields), jnp.float32),
            jax.ShapeDtypeStruct((total, fields), jnp.float32),
            jax.ShapeDtypeStruct((16, fields), jnp.float32),
        ),
        in_specs=[pl.BlockSpec(memory_space=pltpu.SMEM)] + [vmem] * 6,
        out_specs=(vmem, vmem, vmem),
        scratch_shapes=[
            pltpu.VMEM((2, total, fields), jnp.bfloat16),
            pltpu.VMEM((2, 3, blocks, total, fields), jnp.bfloat16),
            pltpu.VMEM((blocks, total, fields), jnp.float32),
            pltpu.VMEM((coefs, 2 * fields), jnp.float32),
            pltpu.VMEM((3 * spheres, coefs, 2 * fields), jnp.bfloat16),
            pltpu.VMEM((2, shard_count, ROWS, fields), jnp.bfloat16),
            pltpu.VMEM((2, quads, per_quad, ROWS, fields), jnp.bfloat16),
            pltpu.VMEM((2, line_size, per_quad, ROWS, fields), jnp.bfloat16),
            pltpu.VMEM((2, shard_count, ROWS, fields), jnp.bfloat16),
            pltpu.VMEM((4, max(quads, line_size), 8, fields), jnp.float32),
            pltpu.VMEM((total, fields), jnp.float32),
            pltpu.SemaphoreType.DMA((46,)),
            pltpu.SemaphoreType.DMA((24,)),
            pltpu.SemaphoreType.DMA((2, 3, blocks)),
        ],
        compiler_params=pltpu.CompilerParams(collective_id=0, has_side_effects=True),
        name="arnoldi",
    )(sources, start, gather, spread, trig, mie, trans)

    def unpacked(field):
        return field.reshape(spheres, rows, 2, fields).transpose(0, 2, 1, 3)

    return unpacked(basis), unpacked(residual), hess[:9]


def solution(mesh):
    highs = 4 if mesh.shape[SLAB] % 4 == 0 and mesh.shape[SLAB] > 4 else 2
    quads = mesh.shape[SLAB] // highs
    return jax.shard_map(
        functools.partial(per_device, quads, highs),
        mesh=mesh,
        in_specs=(
            P(SLAB, None, BLK, None),
            P(SLAB, None, BLK),
            P(SLAB, None, None, BLK, None),
            P(SLAB, None),
            P(SLAB, None),
            P(SLAB, None),
            P(),
            P(),
            P(),
        ),
        out_specs=(P(SLAB, None, BLK, None), P(SLAB, None, BLK, None), P()),
        check_vma=False,
    )
```

time: 844 us -> 95.4 us (0.11)
  waiting for transfers between devices: 529 us -> 0 us
  blocking collectives: 227 us -> 0 us
  Pallas kernels: 0 us -> 77.4 us
  starting transfers between devices: 31.5 us -> 0 us
  between operations: 14.6 us -> 0.73 us
  matrix products: 10.6 us -> 0 us
    psum x2 -> x0, waiting for transfers between devices: 525 us -> none  [apply_operator(): totals = lax.psum(plane_sums(projected, cos_part, sin_part), SLAB_BLK)]
    psum x25 -> x0, blocking collectives: 227 us -> none  [over_axes(): value = lax.psum(value, axis)]
    pallas_call x0 -> x1, Pallas kernels: none -> 77.4 us  [per_device(): pl.pallas_call(functools.partial(kernel, quads, highs, spheres, pairs, co...]
    ppermute x4 -> x0, starting transfers between devices: 23.2 us -> none  [the longest x2 18.7 us: with_halo(): lax.ppermute(head, axis, [((i + 1) % count, i) for i in range(count)])]
    dot_general x6 -> x0, matrix products: 10.6 us -> none  [the longest x2 5.61 us: apply_operator(): jnp.einsum('parc,pzcn->pazrn', flat_trans, sources, preferred_element_typ...]
  transfers between devices with their start and end apart: 8 -> 0, of which waited for: 5 -> 0; matrix products, arithmetic and copies ran while one was open for 2% -> 0% of each run, Pallas kernels for 0% -> 0%
where the time goes in v1:
time: 95.4 us; the launch traced here: 95 us
  Pallas kernels  77.4 us (81%)
  local copies, waits for them, and re-layouts  13.6 us (14%)
  other arithmetic  3.25 us (3%)
    pallas_call x1, Pallas kernels, per_device(): pl.pallas_call(functools.partial(kernel, quads, highs, spheres, pairs, co...  77.4 us
    unnamed x8, local copies, waits for them, and re-layouts  5.27 us
    reshape x1, local copies, waits for them, and re-layouts, per_device(): translation.transpose(0, 1, 3, 2, 4)  2.87 us

profile of v1, /device:TPU:1, one launch (start us, length us, event | category | flops | bytes accessed | tf_op | source)
XLA Modules:
  0.0 95.0 jit_solution(3768232949962577096)
XLA Ops:
  0.6 0.0 copy-start
  0.6 0.8 multiply_add_fusion
  1.5 0.6 reshape.36.source_ref
  2.1 0.8 copy.30
  2.8 0.8 slice_reduce_fusion
  3.6 0.1 reshape_squeeze.3
  3.7 0.7 convert_element_type.3
  4.4 0.1 multiply_reduce_fusion
  4.5 0.1 multiply_cosine_fusion
  4.5 0.7 pad_maximum_fusion.1
  5.2 0.8 dynamic-slice_bitcast_fusion.1
  6.1 0.1 broadcast_in_dim.9
  6.1 0.1 stack_reshape.6
  6.3 0.1 copy.31
  6.4 0.2 stack_reshape.7
  6.6 0.8 fusion
  7.5 0.1 copy.29
  7.6 0.1 reshape.38.spread_ref
  7.7 0.0 copy-start.1
  7.7 0.8 copy.33.trig_ref
  8.5 0.8 copy.34.mie_ref
  9.3 0.9 copy.32.gather_ref
  10.2 0.0 copy-done
  10.2 2.9 %reshape.39.trans_ref = bf16[16,168,336]{2,1,0:T(8,128)(2,1)} reshape(bf16[2,8,84,2,336]{4,3,2,1,0:T(2,128)(2,1)S(1)} %bitcast.27) | data formatting | bytes 3612672 | tf_op jit(solution)/shard_map/reshape | solution.py:513
  13.1 0.0 copy-done.1
  13.1 77.4 %arnoldi.1 = (f32[336,128]{1,0:T(8,128)}, f32[336,128]{1,0:T(8,128)}, f32[16,128]{1,0:T(8,128)}) custom-call(s32[16]{0:T(128)} %reshape.36.source_ref, f32[336,128]{1,0:T(8,128)} %bitcast.31, bf16[512,168]{1,0:T(8,128)(2,1)} %copy.32.gather_ref, bf16[168,512]{1,0:T(8,128)(2,1)} %copy-done.1, f32[256,5]{1,0:T(8,128)} %copy.33.trig_ref, ...), custom_call_target="tpu_custom_call" | custom-call | tf_op jit(solution)/shard_map/arnoldi/pallas_call | solution.py:535
  90.5 1.6 %copy.38 = f32[2,2,84,128]{3,1,2,0:T(2,128)} copy(f32[2,2,84,128]{3,1,2,0:T(2,128)} %bitcast.30) | data formatting | bytes 344064
  92.1 1.6 %copy.39 = f32[2,2,84,128]{3,1,2,0:T(2,128)} copy(f32[2,2,84,128]{3,1,2,0:T(2,128)} %bitcast.29) | data formatting | bytes 344064
  93.7 1.3 %copy.40 = f32[9,128]{1,0:T(8,128)} copy(f32[9,128]{1,0:T(8,128)} %bitcast.34) | data formatting | bytes 9216
  (5 shorter events, 0.1 us)
Async XLA Ops:
  0.6 9.5 %copy-start = (bf16[2,8,2,84,336]{4,2,3,1,0:T(2,128)(2,1)S(1)}, bf16[2,8,2,84,336]{4,2,3,1,0:T(2,128)(2,1)}, u32[]{:S(2)}) copy-start(bf16[2,8,2,84,336]{4,2,3,1,0:T(2,128)(2,1)} %param.11) | copy-start | bytes 5419012
  7.7 5.4 %copy-start.1 = (bf16[168,512]{1,0:T(8,128)(2,1)}, bf16[168,512]{1,0:T(8,128)(2,1)S(1)}, u32[]{:S(2)}) copy-start(bf16[168,512]{1,0:T(8,128)(2,1)S(1)} %reshape.38.spread_ref) | copy-start | bytes 516100

commit v2 on v1

--- a/solution.py
+++ b/solution.py
@@ -39,16 +39,27 @@
     pairs,
     coefs,
     entries,
-    source_ref,
+    shift_ref,
+    member_ref,
+    position_ref,
+    wave_ref,
+    weight_ref,
+    mie_in_ref,
+    start_hbm,
+    plane_hbm,
+    trans_hbm,
+    image_hbm,
+    second_hbm,
+    out_ref,
     start_ref,
+    plane_ref,
+    trans_ref,
     gather_ref,
     spread_ref,
     trig_ref,
     mie_ref,
-    trans_ref,
-    next_ref,
-    residual_ref,
-    hess_ref,
+    image_ref,
+    second_ref,
     piece_ref,
     halo_ref,
     stage_ref,
@@ -63,6 +74,7 @@
     send_sem,
     recv_sem,
     halo_sem,
+    load_sem,
 ):
     blocks = 4
     slabs = quads * highs
@@ -78,24 +90,45 @@
     wide = 2 * rows
     total = spheres * wide
     waves = gather_ref.shape[0] // 2
+    loads = [
+        pltpu.make_async_copy(src, dst, load_sem.at[number])
+        for number, (src, dst) in enumerate(
+            ((plane_hbm, plane_ref), (start_hbm, start_ref), (trans_hbm, trans_ref))
+        )
+    ]
+    for load in loads:
+        load.start()
+
+    def far_first(step, size):
+        half = (step + 1) // 2
+        return lax.rem(size // 2 + jnp.where(lax.rem(step, 2) == 1, -half, half), size)
+
+    ring_x = 4 if quads == 32 else 1
+    ring_z = quads // ring_x
+
+    def plane_quad(step):
+        place_x = lax.rem(quad // ring_z + far_first(lax.rem(step, ring_x), ring_x), ring_x)
+        place_z = lax.rem(lax.rem(quad, ring_z) + far_first(step // ring_x, ring_z), ring_z)
+        return place_x * ring_z + place_z
 
     def plane_peer(step):
-        return (lax.rem(quad + step, quads) * highs + high, blk)
+        return (plane_quad(step) * highs + high, blk)
 
     def line_peer(step):
-        other = lax.rem(spot + step, line_size)
-        return (quad * highs + other // blocks, lax.rem(other, blocks))
+        place = lax.rem(2 * high + low + far_first(step // 2, 2 * highs), 2 * highs)
+        side = lax.rem(core + 1 - lax.rem(step, 2), 2)
+        return (quad * highs + place // 2, lax.rem(place, 2) * 2 + side)
 
     def shifted(step):
         return lax.rem(slab + step + slabs, slabs)
 
     barrier = pltpu.get_barrier_semaphore()
 
-    @pl.loop(1, quads)
+    @pl.loop(0, quads - 1)
     def _(step):
         pl.semaphore_signal(barrier, inc=1, device_id=plane_peer(step), device_id_type=MESH)
 
-    @pl.loop(1, line_size)
+    @pl.loop(0, line_size - 1)
     def _(step):
         pl.semaphore_signal(barrier, inc=1, device_id=line_peer(step), device_id_type=MESH)
 
@@ -130,7 +163,7 @@
         own = piece_ref.at[turn]
         out = []
         slot = 24 + 11 * turn
-        for step, side in ((1, 0), (1, 1), (-1, 0), (-1, 1)):
+        for step, side in ((1, 1), (-1, 0), (1, 0), (-1, 1)):
             out.append(
                 send(
                     own,
@@ -169,7 +202,7 @@
         return out
 
     def exchange(src_of, dst, turn_slot, peer, size):
-        @pl.loop(1, size)
+        @pl.loop(0, size - 1)
         def _(step):
             send(src_of(step), dst, recv_sem.at[turn_slot], turn_slot, peer(step)).start()
 
@@ -217,7 +250,7 @@
 
     def start_scatter(turn):
         exchange(
-            lambda step: shards_of(cut_ref, turn, lax.rem(quad + step, quads)),
+            lambda step: shards_of(cut_ref, turn, plane_quad(step)),
             part_ref.at[turn, quad],
             10 * turn + 2,
             plane_peer,
@@ -288,9 +321,10 @@
         total_product = jnp.zeros((wide, 256), jnp.float32)
         for pair in range(pairs):
             number = sphere * pairs + pair
+            source = (shift_ref[sphere, pair] + 1) * spheres + member_ref[sphere, pair]
             total_product = total_product + jnp.dot(
-                trans_ref[number],
-                joined_ref[source_ref[number]],
+                trans_ref[number].reshape(wide, coefs),
+                joined_ref[source],
                 preferred_element_type=jnp.float32,
             )
         swapped = pair_swap(total_product[:, 128:], even)
@@ -329,8 +363,12 @@
             for side in (0, 1):
                 arrived(place, side)
             join(turn, place)
+        if turn == 0:
+            loads[2].wait()
         for sphere in range(spheres):
             near_field(sphere)
+        if turn == 0:
+            spread_mie()
         finish_gather(turn)
         far = far_field(turn)
         out = []
@@ -338,9 +376,57 @@
             span = slice(sphere * wide, (sphere + 1) * wide)
             summed = near_ref[span] + far[:, 128 * sphere : 128 * (sphere + 1)]
             swapped = pair_swap(summed, even)
-            out.append(mie_ref[span, 0:1] * summed + mie_ref[span, 1:2] * swapped)
+            out.append(mie_ref[0, span] * summed + mie_ref[1, span] * swapped)
         return out, halo, forward
 
+    def make_trig():
+        cos_rows, sin_rows = [], []
+        for sphere in range(spheres):
+            turns = jnp.zeros((1, waves), jnp.float32)
+            for axis in range(3):
+                turns = turns + wave_ref[axis : axis + 1, :].astype(jnp.float32) * (
+                    position_ref[sphere, axis]
+                )
+            angle = two_pi * (turns - jnp.round(turns))
+            cos_rows.append(jnp.cos(angle))
+            sin_rows.append(jnp.sin(angle))
+        lines = cos_rows + sin_rows + [weight_ref[...]]
+        lines.append(jnp.zeros((128 - len(lines), waves), jnp.float32))
+        trig_ref[...] = jnp.concatenate(lines, axis=0).T
+
+    def make_plane():
+        upper = jnp.concatenate([plane_ref[0], plane_ref[1]], axis=1)
+        lower = jnp.concatenate([-plane_ref[1], plane_ref[0]], axis=1)
+        row = lax.broadcasted_iota(jnp.int32, (wide, coefs), 0)
+        hit = lax.broadcasted_iota(jnp.int32, (wide, coefs), 1) == blk * rows + row // 2
+        real = jnp.where(hit & (row % 2 == 0), 1.0, 0.0).astype(jnp.bfloat16)
+        imag = jnp.where(hit & (row % 2 == 1), 1.0, 0.0).astype(jnp.bfloat16)
+        own = jnp.dot(real, upper, preferred_element_type=jnp.float32) + jnp.dot(
+            imag, lower, preferred_element_type=jnp.float32
+        )
+        spread_ref[...] = own.astype(jnp.bfloat16)
+        gather_ref[...] = own.T.astype(jnp.bfloat16)
+
+    def spread_mie():
+        lines = jnp.concatenate(
+            [mie_in_ref[sphere] for sphere in range(spheres)]
+            + [jnp.zeros((128 - 2 * spheres, rows), jnp.float32)],
+            axis=0,
+        )
+        lines = jnp.concatenate([lines, jnp.zeros((128, 128 - rows), jnp.float32)], axis=1).T
+        for sphere in range(spheres):
+            real = jnp.broadcast_to(lines[:rows, 2 * sphere : 2 * sphere + 1], (rows, 128))
+            imag = jnp.broadcast_to(lines[:rows, 2 * sphere + 1 : 2 * sphere + 2], (rows, 128))
+            base = sphere * wide
+            mie_ref[0, pl.ds(base, rows, stride=2), :] = real
+            mie_ref[0, pl.ds(base + 1, rows, stride=2), :] = real
+            mie_ref[1, pl.ds(base, rows, stride=2), :] = -imag
+            mie_ref[1, pl.ds(base + 1, rows, stride=2), :] = imag
+
+    make_trig()
+    loads[0].wait()
+    make_plane()
+    loads[1].wait()
     start = [start_ref[sphere * wide : (sphere + 1) * wide] for sphere in range(spheres)]
     make_piece(0, start_ref)
     first_sums = project(start_ref[...])
@@ -388,14 +474,20 @@
         return gram_ref[slot + 1, pl.ds(0, quads)].sum(axis=0)
 
     for sphere in range(spheres):
-        next_ref[pl.ds(sphere * wide, wide), :] = image[sphere]
-    make_piece(1, next_ref)
-    second_sums = project(next_ref[...])
+        image_ref[pl.ds(sphere * wide, wide), :] = image[sphere]
+    make_piece(1, image_ref)
+    second_sums = project(image_ref[...])
+    store_image = pltpu.make_async_copy(image_ref, image_hbm, load_sem.at[3])
+    store_image.start()
     put_gram(0, (("real", start, start), ("complex", start, image), ("real", image, image)))
     start_gram(0, 20)
-    second, halo_two, forward_two = operator(1, next_ref, second_sums)
+    second, halo_two, forward_two = operator(1, image_ref, second_sums)
     put_gram(2, (("complex", start, second), ("complex", image, second), ("real", second, second)))
     start_gram(2, 22)
+    for sphere in range(spheres):
+        second_ref[pl.ds(sphere * wide, wide), :] = second[sphere]
+    store_second = pltpu.make_async_copy(second_ref, second_hbm, load_sem.at[4])
+    store_second.start()
     turn_gram(0, 20)
     turn_gram(2, 22)
     early = end_gram(0, 20)
@@ -447,32 +539,13 @@
         + 2.0 * scale * (y_re * e_re + y_im * e_im)
     )
     h32 = jnp.sqrt(jnp.maximum(left, 0.0) / entries + epsilon)
-    hess_ref[...] = jnp.concatenate(
-        [
-            beta,
-            h11_re,
-            h11_im,
-            h21,
-            h12_re,
-            h12_im,
-            h22_re,
-            h22_im,
-            h32,
-            jnp.zeros((7, 128), jnp.float32),
-        ],
+    out_ref[...] = jnp.concatenate(
+        [beta, h11_re, h11_im, h21, h12_re, h12_im, h22_re, h22_im, h32]
+        + [a_re, a_im, x_re, x_im, y_re, y_im, scale, jnp.zeros((8, 128), jnp.float32)],
         axis=0,
     )
-    for sphere in range(spheres):
-        span = pl.ds(sphere * wide, wide)
-        one = start_ref[span, :]
-        two = next_ref[span, :]
-        one_swapped, two_swapped = pair_swap(one, even), pair_swap(two, even)
-        residual_ref[span, :] = (
-            complex_rows(x_re, x_im, one, one_swapped, even)
-            + complex_rows(y_re, y_im, two, two_swapped, even)
-            + scale * second[sphere]
-        )
-        next_ref[span, :] = complex_rows(a_re, a_im, one, one_swapped, even) - scale * two
+    store_image.wait()
+    store_second.wait()
 
     for copy in halo_one + forward_one + halo_two + forward_two:
         copy.wait_send()
@@ -486,6 +559,28 @@
     for slot in (0, 2):
         drain(gram_ref.at[slot], 20 + slot, line_size, "send")
         drain(gram_ref.at[slot + 1], 21 + slot, quads, "send")
+
+
+def combine_kernel(
+    spheres, scalar_ref, start_ref, image_ref, second_ref, next_ref, residual_ref, hess_ref
+):
+    wide = start_ref.shape[0] // spheres
+    even = (lax.broadcasted_iota(jnp.int32, (wide, 128), 0) % 2) == 0
+    hess_ref[...] = scalar_ref[0:9, :]
+    a_re, a_im, x_re, x_im, y_re, y_im, scale = (
+        scalar_ref[9 + number : 10 + number, :] for number in range(7)
+    )
+    for sphere in range(spheres):
+        span = pl.ds(sphere * wide, wide)
+        one = start_ref[span, :]
+        two = image_ref[span, :]
+        one_swapped, two_swapped = pair_swap(one, even), pair_swap(two, even)
+        next_ref[span, :] = complex_rows(a_re, a_im, one, one_swapped, even) - scale * two
+        residual_ref[span, :] = (
+            complex_rows(x_re, x_im, one, one_swapped, even)
+            + complex_rows(y_re, y_im, two, two_swapped, even)
+            + scale * second_ref[span, :]
+        )
 
 
 def per_device(
@@ -510,38 +605,28 @@
     blocks = coefs // rows
     line_size = highs * blocks
     start = incident.transpose(0, 2, 1, 3).reshape(total, fields)
-    trans = translation.transpose(0, 1, 3, 2, 4).reshape(spheres * pairs, 2 * rows, coefs)
-    sources = ((pair_shift + 1) * spheres + pair_member).reshape(-1)
-    angles = two_pi * jnp.sum(
-        wave_index.astype(jnp.float32)[:, None, :] * positions[None, :, :], axis=-1
-    )
-    trig = jnp.concatenate([jnp.cos(angles), jnp.sin(angles), ewald_weight[:, None]], axis=1)
-    mie_re = jnp.repeat(mie_coef[:, 0].reshape(-1), 2)
-    mie_im = jnp.stack([-mie_coef[:, 1], mie_coef[:, 1]], axis=-1).reshape(-1)
-    mie = jnp.stack([mie_re, mie_im], axis=1)
-    coef_rows = lax.dynamic_slice_in_dim(plane_coef, lax.axis_index(BLK) * rows, rows, 2)
-    coef_re, coef_im = coef_rows[:, 0].T, coef_rows[:, 1].T
-    spread = jnp.stack(
-        [
-            jnp.concatenate([coef_re, coef_im], axis=1),
-            jnp.concatenate([-coef_im, coef_re], axis=1),
-        ],
-        axis=1,
-    ).reshape(2 * rows, 2 * waves)
-    gather = spread.T
+    trans = translation.transpose(0, 1, 3, 2, 4).reshape(spheres * pairs, rows, 2, coefs)
     shard_count = 2 * waves // ROWS
     per_quad = shard_count // quads
     vmem = pl.BlockSpec(memory_space=pltpu.VMEM)
-    basis, residual, hess = pl.pallas_call(
+    smem = pl.BlockSpec(memory_space=pltpu.SMEM)
+    hbm = pl.BlockSpec(memory_space=pl.ANY)
+    vector = jax.ShapeDtypeStruct((total, fields), jnp.float32)
+    image, second, scalars = pl.pallas_call(
         functools.partial(kernel, quads, highs, spheres, pairs, coefs, entries),
-        out_shape=(
-            jax.ShapeDtypeStruct((total, fields), jnp.float32),
-            jax.ShapeDtypeStruct((total, fields), jnp.float32),
-            jax.ShapeDtypeStruct((16, fields), jnp.float32),
-        ),
-        in_specs=[pl.BlockSpec(memory_space=pltpu.SMEM)] + [vmem] * 6,
-        out_specs=(vmem, vmem, vmem),
+        out_shape=(vector, vector, jax.ShapeDtypeStruct((24, fields), jnp.float32)),
+        in_specs=[smem, smem, smem, vmem, vmem, vmem, hbm, hbm, hbm],
+        out_specs=(hbm, hbm, vmem),
         scratch_shapes=[
+            pltpu.VMEM((total, fields), jnp.float32),
+            pltpu.VMEM((2, coefs, waves), jnp.bfloat16),
+            pltpu.VMEM((spheres * pairs, rows, 2, coefs), jnp.bfloat16),
+            pltpu.VMEM((2 * waves, 2 * rows), jnp.bfloat16),
+            pltpu.VMEM((2 * rows, 2 * waves), jnp.bfloat16),
+            pltpu.VMEM((waves, 128), jnp.float32),
+            pltpu.VMEM((2, total, fields), jnp.float32),
+            pltpu.VMEM((total, fields), jnp.float32),
+            pltpu.VMEM((total, fields), jnp.float32),
             pltpu.VMEM((2, total, fields), jnp.bfloat16),
             pltpu.VMEM((2, 3, blocks, total, fields), jnp.bfloat16),
             pltpu.VMEM((blocks, total, fields), jnp.float32),
@@ -556,15 +641,33 @@
             pltpu.SemaphoreType.DMA((46,)),
             pltpu.SemaphoreType.DMA((24,)),
             pltpu.SemaphoreType.DMA((2, 3, blocks)),
+            pltpu.SemaphoreType.DMA((5,)),
         ],
         compiler_params=pltpu.CompilerParams(collective_id=0, has_side_effects=True),
         name="arnoldi",
-    )(sources, start, gather, spread, trig, mie, trans)
+    )(
+        pair_shift,
+        pair_member,
+        positions,
+        wave_index.T,
+        ewald_weight.reshape(1, waves),
+        mie_coef,
+        start,
+        plane_coef.transpose(1, 2, 0),
+        trans,
+    )
+    basis, residual, hess = pl.pallas_call(
+        functools.partial(combine_kernel, spheres),
+        out_shape=(vector, vector, jax.ShapeDtypeStruct((9, fields), jnp.float32)),
+        in_specs=[vmem] * 4,
+        out_specs=(vmem, vmem, vmem),
+        name="combine",
+    )(scalars, start, image, second)
 
     def unpacked(field):
         return field.reshape(spheres, rows, 2, fields).transpose(0, 2, 1, 3)
 
-    return unpacked(basis), unpacked(residual), hess[:9]
+    return unpacked(basis), unpacked(residual), hess
 
 
 def solution(mesh):

time: 95.4 us -> 76.8 us (0.81)
  local copies, waits for them, and re-layouts: 13.6 us -> 0 us
  other arithmetic: 3.25 us -> 0 us
  Pallas kernels: 77.4 us -> 76 us
    unnamed x8 -> x0, local copies, waits for them, and re-layouts: 5.27 us -> none
    reshape x3 -> x0, local copies, waits for them, and re-layouts: 3.53 us -> none  [the longest x1 2.87 us: per_device(): translation.transpose(0, 1, 3, 2, 4)]
    pallas_call x1, Pallas kernels: 77.4 us -> 74.1 us  [per_device(): pl.pallas_call(functools.partial(kernel, quads, highs, spheres, pairs, co...]
    pallas_call x0 -> x1, Pallas kernels: none -> 1.97 us  [per_device(): pl.pallas_call(functools.partial(combine_kernel, spheres), out_shape=(vec...]
    transpose x2 -> x0, local copies, waits for them, and re-layouts: 1.67 us -> none  [the longest x1 0.86 us: per_device(): gather = spread.T]
    another operation x6 -> x0, local copies, waits for them, and re-layouts: 1.46 us -> none  [the longest x3 1.11 us: per_device(): mie = jnp.stack([mie_re, mie_im], axis=1)]
where the time goes in v2:
time: 76.8 us; the launch traced here: 76.7 us
  Pallas kernels  76 us (99%)
    pallas_call x1, Pallas kernels, per_device(): pl.pallas_call(functools.partial(kernel, quads, highs, spheres, pairs, co...  74.1 us
    pallas_call x1, Pallas kernels, per_device(): pl.pallas_call(functools.partial(combine_kernel, spheres), out_shape=(vec...  1.97 us

profile of v2, /device:TPU:1, one launch (start us, length us, event | category | flops | bytes accessed | tf_op | source)
XLA Modules:
  0.0 76.7 jit_solution(13702466100220219783)
XLA Ops:
  0.6 74.1 %arnoldi.1 = (f32[336,128]{1,0:T(8,128)}, f32[336,128]{1,0:T(8,128)}, f32[24,128]{1,0:T(8,128)}) custom-call(s32[2,8]{1,0:T(2,128)} %shift_ref.1, s32[2,8]{1,0:T(2,128)} %member_ref.1, f32[2,3]{1,0:T(2,128)} %position_ref.1, s32[3,256]{1,0:T(4,128)} %bitcast.19, f32[1,256]{1,0:T(1,128)} %bitcast.20, f32[2,2,84]{2,1,0:T(2,128)} %mie_in_ref.1, ...), custom_call_target="tpu_custom_call" | custom-call | tf_op jit(solution)/shard_map/arnoldi/pallas_call | solution.py:615
  74.7 2.0 %combine.1 = (f32[336,128]{1,0:T(8,128)}, f32[336,128]{1,0:T(8,128)}, f32[9,128]{1,0:T(8,128)}) custom-call(f32[24,128]{1,0:T(8,128)} %get-tuple-element.9.scalar_ref, f32[336,128]{1,0:T(8,128)} %bitcast.17, f32[336,128]{1,0:T(8,128)} %get-tuple-element.10.image_ref, f32[336,128]{1,0:T(8,128)} %get-tuple-element.11.second_ref), custom_call_target="tpu_custom_call" | custom-call | tf_op jit(solution)/shard_map/combine/pallas_call | solution.py:659

commit v3 on v2

--- a/solution.py
+++ b/solution.py
@@ -48,18 +48,16 @@
     start_hbm,
     plane_hbm,
     trans_hbm,
-    image_hbm,
-    second_hbm,
+    start_ref,
+    image_ref,
+    second_ref,
     out_ref,
-    start_ref,
     plane_ref,
     trans_ref,
     gather_ref,
     spread_ref,
     trig_ref,
     mie_ref,
-    image_ref,
-    second_ref,
     piece_ref,
     halo_ref,
     stage_ref,
@@ -119,9 +117,6 @@
         side = lax.rem(core + 1 - lax.rem(step, 2), 2)
         return (quad * highs + place // 2, lax.rem(place, 2) * 2 + side)
 
-    def shifted(step):
-        return lax.rem(slab + step + slabs, slabs)
-
     barrier = pltpu.get_barrier_semaphore()
 
     @pl.loop(0, quads - 1)
@@ -132,12 +127,13 @@
     def _(step):
         pl.semaphore_signal(barrier, inc=1, device_id=line_peer(step), device_id_type=MESH)
 
+    def chain_peer(step):
+        place = lax.rem(2 * slab + low + step + 2 * slabs, 2 * slabs)
+        return (place // 2, lax.rem(place, 2) * 2 + core)
+
     for step in (-1, 1):
-        for side in (0, 1):
-            pl.semaphore_signal(
-                barrier, inc=1, device_id=(shifted(step), side * 2 + core), device_id_type=MESH
-            )
-    greeted = quads - 1 + line_size - 1 + 4
+        pl.semaphore_signal(barrier, inc=1, device_id=chain_peer(step), device_id_type=MESH)
+    greeted = quads - 1 + line_size - 1 + 2
 
     even = (lax.broadcasted_iota(jnp.int32, (wide, 128), 0) % 2) == 0
 
@@ -159,47 +155,43 @@
             device_id_type=MESH,
         )
 
+    partner = (slab, low * 2 + 1 - core)
+
+    def slot_of(turn, offset, viewer=0):
+        place = (low + offset + 4) // 2 - (low + viewer + 4) // 2 + 1
+        return turn, place, lax.rem(low + offset + 4, 2) * 2 + core
+
+    def relay(turn, offset, step, number):
+        target = slot_of(turn, offset, step)
+        src = piece_ref.at[turn] if number < 2 else halo_ref.at[slot_of(turn, offset)]
+        return send(
+            src, halo_ref.at[target], halo_sem.at[target], 24 + 11 * turn + number, chain_peer(step)
+        )
+
+    def share(turn, offset, number):
+        slot = slot_of(turn, offset)
+        src = piece_ref.at[turn] if number == 5 else halo_ref.at[slot]
+        return send(src, halo_ref.at[slot], halo_sem.at[slot], 24 + 11 * turn + number, partner)
+
+    def arrive(turn, offset):
+        slot = slot_of(turn, offset)
+        ref = halo_ref.at[slot]
+        send(ref, ref, halo_sem.at[slot], 24 + 11 * turn, partner).wait_recv()
+
+    toward = 1 - 2 * low
+
     def halo_copies(turn):
-        own = piece_ref.at[turn]
-        out = []
-        slot = 24 + 11 * turn
-        for step, side in ((1, 1), (-1, 0), (1, 0), (-1, 1)):
-            out.append(
-                send(
-                    own,
-                    halo_ref.at[turn, 1 - step, blk],
-                    halo_sem.at[turn, 1 - step, blk],
-                    slot + len(out),
-                    (shifted(step), side * 2 + core),
-                )
-            )
-        for device in ((slab, (1 - low) * 2 + core), (slab, low * 2 + 1 - core)):
-            out.append(
-                send(
-                    own,
-                    halo_ref.at[turn, 1, blk],
-                    halo_sem.at[turn, 1, blk],
-                    slot + len(out),
-                    device,
-                )
-            )
-        return out
-
-    def forward_copies(turn):
-        out = []
-        slot = 30 + 11 * turn
-        for place, side in ((1, 1 - low), (0, 0), (0, 1), (2, 0), (2, 1)):
-            index = side * 2 + core
-            out.append(
-                send(
-                    halo_ref.at[turn, place, index],
-                    halo_ref.at[turn, place, index],
-                    halo_sem.at[turn, place, index],
-                    slot + len(out),
-                    (slab, low * 2 + 1 - core),
-                )
-            )
-        return out
+        return (
+            [relay(turn, 0, 1, 0), relay(turn, 0, -1, 1), relay(turn, -1, 1, 2)]
+            + [relay(turn, 1, -1, 3), relay(turn, -2 * toward, toward, 4), share(turn, 0, 5)]
+            + [share(turn, -1, 6), share(turn, 1, 7), share(turn, -2, 8), share(turn, 2, 9)]
+            + [share(turn, 3 * toward, 10)]
+        )
+
+    def start_halo(turn):
+        copies = halo_copies(turn)
+        for number in (0, 1, 5):
+            copies[number].start()
 
     def exchange(src_of, dst, turn_slot, peer, size):
         @pl.loop(0, size - 1)
@@ -335,33 +327,30 @@
     def operator(turn, source, sums):
         cut(turn, sums)
         start_scatter(turn)
-        halo = halo_copies(turn)
-        for copy in halo:
-            copy.start()
+        copies = halo_copies(turn)
         halo_ref[turn, 1, blk] = piece_ref[turn]
+        for offset, numbers in ((-1, (2, 6)), (1, (3, 7))):
+            arrive(turn, offset)
+            for number in numbers:
+                copies[number].start()
         finish_scatter(turn)
         start_line(turn)
-        forward = forward_copies(turn)
-        for copy in forward:
-            copy.wait_recv()
-            copy.start()
-        other = 1 - core
-
-        def arrived(place, side):
-            index = side * 2 + other
-            send(
-                halo_ref.at[turn, place, index],
-                halo_ref.at[turn, place, index],
-                halo_sem.at[turn, place, index],
-                10 * turn + 1,
-                (slab, blk),
-            ).wait_recv()
-
+        arrive(turn, -2 * toward)
+        copies[4].start()
+        arrive(turn, 2 * toward)
+        for number in (8, 9):
+            copies[number].start()
         finish_line(turn)
         start_gather(turn)
+        if turn == 1:
+            turn_gram(0, 20)
+        arrive(turn, 3 * toward)
+        copies[10].start()
         for place in (1, 0, 2):
             for side in (0, 1):
-                arrived(place, side)
+                index = side * 2 + 1 - core
+                ref = halo_ref.at[turn, place, index]
+                send(ref, ref, halo_sem.at[turn, place, index], 24 + 11 * turn, partner).wait_recv()
             join(turn, place)
         if turn == 0:
             loads[2].wait()
@@ -377,7 +366,7 @@
             summed = near_ref[span] + far[:, 128 * sphere : 128 * (sphere + 1)]
             swapped = pair_swap(summed, even)
             out.append(mie_ref[0, span] * summed + mie_ref[1, span] * swapped)
-        return out, halo, forward
+        return out
 
     def make_trig():
         cos_rows, sin_rows = [], []
@@ -431,7 +420,8 @@
     make_piece(0, start_ref)
     first_sums = project(start_ref[...])
     pl.semaphore_wait(barrier, greeted)
-    image, halo_one, forward_one = operator(0, start_ref, first_sums)
+    start_halo(0)
+    image = operator(0, start_ref, first_sums)
 
     def put_gram(slot, pairs_of):
         lines = []
@@ -447,48 +437,53 @@
         lines.append(jnp.zeros((8 - len(lines), 128), jnp.float32))
         gram_ref[slot, spot] = jnp.concatenate(lines, axis=0)
 
+    def lines_of(slot, place):
+        return gram_ref.at[slot, place, pl.ds(0, 4 if slot < 2 else 5)]
+
     def start_gram(slot, turn_slot):
         exchange(
-            lambda step: gram_ref.at[slot, spot],
-            gram_ref.at[slot, spot],
+            lambda step: lines_of(slot, spot),
+            lines_of(slot, spot),
             turn_slot,
             line_peer,
             line_size,
         )
 
+    def drain_gram(slot, turn_slot, size, what):
+        ref = gram_ref.at[slot, pl.ds(0, size - 1), pl.ds(0, 4 if slot < 2 else 5)]
+        copy = send(ref, ref, recv_sem.at[turn_slot], turn_slot, (slab, blk))
+        if what == "recv":
+            copy.wait_recv()
+        else:
+            copy.wait_send()
+
     def turn_gram(slot, turn_slot):
-        ref = gram_ref.at[slot, pl.ds(0, line_size - 1)]
-        send(ref, ref, recv_sem.at[turn_slot], turn_slot, (slab, blk)).wait_recv()
+        drain_gram(slot, turn_slot, line_size, "recv")
         gram_ref[slot + 1, quad] = gram_ref[slot, pl.ds(0, line_size)].sum(axis=0)
         exchange(
-            lambda step: gram_ref.at[slot + 1, quad],
-            gram_ref.at[slot + 1, quad],
+            lambda step: lines_of(slot + 1, quad),
+            lines_of(slot + 1, quad),
             turn_slot + 1,
             plane_peer,
             quads,
         )
 
     def end_gram(slot, turn_slot):
-        ref = gram_ref.at[slot + 1, pl.ds(0, quads - 1)]
-        send(ref, ref, recv_sem.at[turn_slot + 1], turn_slot + 1, (slab, blk)).wait_recv()
+        drain_gram(slot + 1, turn_slot + 1, quads, "recv")
         return gram_ref[slot + 1, pl.ds(0, quads)].sum(axis=0)
 
     for sphere in range(spheres):
         image_ref[pl.ds(sphere * wide, wide), :] = image[sphere]
     make_piece(1, image_ref)
+    start_halo(1)
     second_sums = project(image_ref[...])
-    store_image = pltpu.make_async_copy(image_ref, image_hbm, load_sem.at[3])
-    store_image.start()
     put_gram(0, (("real", start, start), ("complex", start, image), ("real", image, image)))
     start_gram(0, 20)
-    second, halo_two, forward_two = operator(1, image_ref, second_sums)
+    second = operator(1, image_ref, second_sums)
     put_gram(2, (("complex", start, second), ("complex", image, second), ("real", second, second)))
     start_gram(2, 22)
     for sphere in range(spheres):
         second_ref[pl.ds(sphere * wide, wide), :] = second[sphere]
-    store_second = pltpu.make_async_copy(second_ref, second_hbm, load_sem.at[4])
-    store_second.start()
-    turn_gram(0, 20)
     turn_gram(2, 22)
     early = end_gram(0, 20)
     late = end_gram(2, 22)
@@ -544,12 +539,10 @@
         + [a_re, a_im, x_re, x_im, y_re, y_im, scale, jnp.zeros((8, 128), jnp.float32)],
         axis=0,
     )
-    store_image.wait()
-    store_second.wait()
-
-    for copy in halo_one + forward_one + halo_two + forward_two:
-        copy.wait_send()
+
     for turn in range(2):
+        for copy in halo_copies(turn):
+            copy.wait_send()
         for slot, size, block in (
             (2, quads, part_ref.at[turn]),
             (3, line_size, line_ref.at[turn]),
@@ -557,8 +550,8 @@
         ):
             drain(block, 10 * turn + slot, size, "send")
     for slot in (0, 2):
-        drain(gram_ref.at[slot], 20 + slot, line_size, "send")
-        drain(gram_ref.at[slot + 1], 21 + slot, quads, "send")
+        drain_gram(slot, 20 + slot, line_size, "send")
+        drain_gram(slot + 1, 21 + slot, quads, "send")
 
 
 def combine_kernel(
@@ -612,21 +605,19 @@
     smem = pl.BlockSpec(memory_space=pltpu.SMEM)
     hbm = pl.BlockSpec(memory_space=pl.ANY)
     vector = jax.ShapeDtypeStruct((total, fields), jnp.float32)
-    image, second, scalars = pl.pallas_call(
+    kept = pltpu.VMEM((total, fields), jnp.float32)
+    first, image, second, scalars = pl.pallas_call(
         functools.partial(kernel, quads, highs, spheres, pairs, coefs, entries),
-        out_shape=(vector, vector, jax.ShapeDtypeStruct((24, fields), jnp.float32)),
+        out_shape=(kept, kept, kept, pltpu.VMEM((24, fields), jnp.float32)),
         in_specs=[smem, smem, smem, vmem, vmem, vmem, hbm, hbm, hbm],
-        out_specs=(hbm, hbm, vmem),
+        out_specs=(vmem, vmem, vmem, vmem),
         scratch_shapes=[
-            pltpu.VMEM((total, fields), jnp.float32),
             pltpu.VMEM((2, coefs, waves), jnp.bfloat16),
             pltpu.VMEM((spheres * pairs, rows, 2, coefs), jnp.bfloat16),
             pltpu.VMEM((2 * waves, 2 * rows), jnp.bfloat16),
             pltpu.VMEM((2 * rows, 2 * waves), jnp.bfloat16),
             pltpu.VMEM((waves, 128), jnp.float32),
             pltpu.VMEM((2, total, fields), jnp.float32),
-            pltpu.VMEM((total, fields), jnp.float32),
-            pltpu.VMEM((total, fields), jnp.float32),
             pltpu.VMEM((2, total, fields), jnp.bfloat16),
             pltpu.VMEM((2, 3, blocks, total, fields), jnp.bfloat16),
             pltpu.VMEM((blocks, total, fields), jnp.float32),
@@ -641,7 +632,7 @@
             pltpu.SemaphoreType.DMA((46,)),
             pltpu.SemaphoreType.DMA((24,)),
             pltpu.SemaphoreType.DMA((2, 3, blocks)),
-            pltpu.SemaphoreType.DMA((5,)),
+            pltpu.SemaphoreType.DMA((3,)),
         ],
         compiler_params=pltpu.CompilerParams(collective_id=0, has_side_effects=True),
         name="arnoldi",
@@ -656,13 +647,17 @@
         plane_coef.transpose(1, 2, 0),
         trans,
     )
+    kept_values = (
+        pltpu.with_memory_space_constraint(value, pltpu.VMEM)
+        for value in (scalars, first, image, second)
+    )
     basis, residual, hess = pl.pallas_call(
         functools.partial(combine_kernel, spheres),
         out_shape=(vector, vector, jax.ShapeDtypeStruct((9, fields), jnp.float32)),
         in_specs=[vmem] * 4,
         out_specs=(vmem, vmem, vmem),
         name="combine",
-    )(scalars, start, image, second)
+    )(*kept_values)
 
     def unpacked(field):
         return field.reshape(spheres, rows, 2, fields).transpose(0, 2, 1, 3)

time: 76.8 us -> 71.7 us (0.934)
  Pallas kernels: 76 us -> 70.9 us
    pallas_call x1, Pallas kernels: 74.1 us -> 70 us  [per_device(): pl.pallas_call(functools.partial(kernel, quads, highs, spheres, pairs, co...]
    pallas_call x1, Pallas kernels: 1.97 us -> 0.87 us  [per_device(): pl.pallas_call(functools.partial(combine_kernel, spheres), out_shape=(vec...]
where the time goes in v3:
time: 71.7 us; the launch traced here: 71.5 us
  Pallas kernels  70.9 us (99%)
    pallas_call x1, Pallas kernels, per_device(): pl.pallas_call(functools.partial(kernel, quads, highs, spheres, pairs, co...  70 us

profile of v3, /device:TPU:1, one launch (start us, length us, event | category | flops | bytes accessed | tf_op | source)
XLA Modules:
  0.0 71.5 jit_solution(6503855217384430033)
XLA Ops:
  0.6 70.0 %arnoldi.1 = (f32[336,128]{1,0:T(8,128)S(1)}, f32[336,128]{1,0:T(8,128)S(1)}, f32[336,128]{1,0:T(8,128)S(1)}, f32[24,128]{1,0:T(8,128)S(1)}) custom-call(s32[2,8]{1,0:T(2,128)} %shift_ref.1, s32[2,8]{1,0:T(2,128)} %member_ref.1, f32[2,3]{1,0:T(2,128)} %position_ref.1, s32[3,256]{1,0:T(4,128)} %bitcast.18, f32[1,256]{1,0:T(1,128)} %bitcast.19, ...), custom_call_target="tpu_custom_call" | custom-call | tf_op jit(solution)/shard_map/arnoldi/pallas_call | solution.py:609
  70.6 0.9 %combine.1 = (f32[336,128]{1,0:T(8,128)}, f32[336,128]{1,0:T(8,128)}, f32[9,128]{1,0:T(8,128)}) custom-call(f32[24,128]{1,0:T(8,128)S(1)} %get-tuple-element.10.scalar_ref, f32[336,128]{1,0:T(8,128)S(1)} %get-tuple-element.11.start_ref, f32[336,128]{1,0:T(8,128)S(1)} %get-tuple-element.12.image_ref, f32[336,128]{1,0:T(8,128)S(1)} %get-tuple-element.13.second_ref), custom_call_target="tpu_custom_call" | custom-call | tf_op jit(solution)/shard_map/combine/pallas_call | solution.py:654

commit v4 on v3

--- a/solution.py
+++ b/solution.py
@@ -39,12 +39,12 @@
     pairs,
     coefs,
     entries,
-    shift_ref,
-    member_ref,
-    position_ref,
-    wave_ref,
-    weight_ref,
-    mie_in_ref,
+    shift_hbm,
+    member_hbm,
+    position_hbm,
+    wave_hbm,
+    weight_hbm,
+    mie_hbm,
     start_hbm,
     plane_hbm,
     trans_hbm,
@@ -73,6 +73,12 @@
     recv_sem,
     halo_sem,
     load_sem,
+    shift_ref,
+    member_ref,
+    position_ref,
+    wave_ref,
+    weight_ref,
+    mie_in_ref,
 ):
     blocks = 4
     slabs = quads * highs
@@ -91,11 +97,19 @@
     loads = [
         pltpu.make_async_copy(src, dst, load_sem.at[number])
         for number, (src, dst) in enumerate(
-            ((plane_hbm, plane_ref), (start_hbm, start_ref), (trans_hbm, trans_ref))
+            (
+                (plane_hbm, plane_ref),
+                (start_hbm, start_ref),
+                (trans_hbm, trans_ref),
+                (position_hbm, position_ref),
+                (wave_hbm, wave_ref),
+                (weight_hbm, weight_ref),
+                (shift_hbm, shift_ref),
+                (member_hbm, member_ref),
+                (mie_hbm, mie_in_ref),
+            )
         )
     ]
-    for load in loads:
-        load.start()
 
     def far_first(step, size):
         half = (step + 1) // 2
@@ -134,6 +148,9 @@
     for step in (-1, 1):
         pl.semaphore_signal(barrier, inc=1, device_id=chain_peer(step), device_id_type=MESH)
     greeted = quads - 1 + line_size - 1 + 2
+
+    for number in (3, 4, 5, 0, 1, 6, 7, 8, 2):
+        loads[number].start()
 
     even = (lax.broadcasted_iota(jnp.int32, (wide, 128), 0) % 2) == 0
 
@@ -325,9 +342,20 @@
         )
 
     def operator(turn, source, sums):
-        cut(turn, sums)
+        if turn == 1:
+            cut(turn, sums)
         start_scatter(turn)
         copies = halo_copies(turn)
+        if turn == 1:
+            put_gram(
+                0,
+                (
+                    ("real", start, start),
+                    ("complex", start, image),
+                    ("real", image, image),
+                ),
+            )
+            start_gram(0, 20)
         halo_ref[turn, 1, blk] = piece_ref[turn]
         for offset, numbers in ((-1, (2, 6)), (1, (3, 7))):
             arrive(turn, offset)
@@ -353,7 +381,8 @@
                 send(ref, ref, halo_sem.at[turn, place, index], 24 + 11 * turn, partner).wait_recv()
             join(turn, place)
         if turn == 0:
-            loads[2].wait()
+            for number in (2, 6, 7, 8):
+                loads[number].wait()
         for sphere in range(spheres):
             near_field(sphere)
         if turn == 0:
@@ -412,6 +441,8 @@
             mie_ref[1, pl.ds(base, rows, stride=2), :] = -imag
             mie_ref[1, pl.ds(base + 1, rows, stride=2), :] = imag
 
+    for number in (3, 4, 5):
+        loads[number].wait()
     make_trig()
     loads[0].wait()
     make_plane()
@@ -419,6 +450,7 @@
     start = [start_ref[sphere * wide : (sphere + 1) * wide] for sphere in range(spheres)]
     make_piece(0, start_ref)
     first_sums = project(start_ref[...])
+    cut(0, first_sums)
     pl.semaphore_wait(barrier, greeted)
     start_halo(0)
     image = operator(0, start_ref, first_sums)
@@ -477,8 +509,6 @@
     make_piece(1, image_ref)
     start_halo(1)
     second_sums = project(image_ref[...])
-    put_gram(0, (("real", start, start), ("complex", start, image), ("real", image, image)))
-    start_gram(0, 20)
     second = operator(1, image_ref, second_sums)
     put_gram(2, (("complex", start, second), ("complex", image, second), ("real", second, second)))
     start_gram(2, 22)
@@ -602,14 +632,13 @@
     shard_count = 2 * waves // ROWS
     per_quad = shard_count // quads
     vmem = pl.BlockSpec(memory_space=pltpu.VMEM)
-    smem = pl.BlockSpec(memory_space=pltpu.SMEM)
     hbm = pl.BlockSpec(memory_space=pl.ANY)
     vector = jax.ShapeDtypeStruct((total, fields), jnp.float32)
     kept = pltpu.VMEM((total, fields), jnp.float32)
     first, image, second, scalars = pl.pallas_call(
         functools.partial(kernel, quads, highs, spheres, pairs, coefs, entries),
         out_shape=(kept, kept, kept, pltpu.VMEM((24, fields), jnp.float32)),
-        in_specs=[smem, smem, smem, vmem, vmem, vmem, hbm, hbm, hbm],
+        in_specs=[hbm] * 9,
         out_specs=(vmem, vmem, vmem, vmem),
         scratch_shapes=[
             pltpu.VMEM((2, coefs, waves), jnp.bfloat16),
@@ -632,7 +661,13 @@
             pltpu.SemaphoreType.DMA((46,)),
             pltpu.SemaphoreType.DMA((24,)),
             pltpu.SemaphoreType.DMA((2, 3, blocks)),
-            pltpu.SemaphoreType.DMA((3,)),
+            pltpu.SemaphoreType.DMA((9,)),
+            pltpu.SMEM(pair_shift.shape, jnp.int32),
+            pltpu.SMEM(pair_member.shape, jnp.int32),
+            pltpu.SMEM(positions.shape, jnp.float32),
+            pltpu.VMEM((3, waves), jnp.int32),
+            pltpu.VMEM((1, waves), jnp.float32),
+            pltpu.VMEM(mie_coef.shape, jnp.float32),
         ],
         compiler_params=pltpu.CompilerParams(collective_id=0, has_side_effects=True),
         name="arnoldi",

time: 71.7 us -> 69.6 us (0.971)
  Pallas kernels: 70.9 us -> 68.9 us
    pallas_call x1, Pallas kernels: 70 us -> 68 us  [per_device(): pl.pallas_call(functools.partial(kernel, quads, highs, spheres, pairs, co...]
where the time goes in v4:
time: 69.6 us; the launch traced here: 69.5 us
  Pallas kernels  68.9 us (99%)
    pallas_call x1, Pallas kernels, per_device(): pl.pallas_call(functools.partial(kernel, quads, highs, spheres, pairs, co...  68 us

profile of v4, /device:TPU:1, one launch (start us, length us, event | category | flops | bytes accessed | tf_op | source)
XLA Modules:
  0.0 69.5 jit_solution(15605018410784813576)
XLA Ops:
  0.6 68.0 %arnoldi.1 = (f32[336,128]{1,0:T(8,128)S(1)}, f32[336,128]{1,0:T(8,128)S(1)}, f32[336,128]{1,0:T(8,128)S(1)}, f32[24,128]{1,0:T(8,128)S(1)}) custom-call(s32[2,8]{1,0:T(2,128)} %shift_hbm.1, s32[2,8]{1,0:T(2,128)} %member_hbm.1, f32[2,3]{1,0:T(2,128)} %position_hbm.1, s32[3,256]{1,0:T(4,128)} %bitcast.18, f32[1,256]{1,0:T(1,128)} %bitcast.19, ...), custom_call_target="tpu_custom_call" | custom-call | tf_op jit(solution)/shard_map/arnoldi/pallas_call | solution.py:638
  68.6 0.9 %combine.1 = (f32[336,128]{1,0:T(8,128)}, f32[336,128]{1,0:T(8,128)}, f32[9,128]{1,0:T(8,128)}) custom-call(f32[24,128]{1,0:T(8,128)S(1)} %get-tuple-element.10.scalar_ref, f32[336,128]{1,0:T(8,128)S(1)} %get-tuple-element.11.start_ref, f32[336,128]{1,0:T(8,128)S(1)} %get-tuple-element.12.image_ref, f32[336,128]{1,0:T(8,128)S(1)} %get-tuple-element.13.second_ref), custom_call_target="tpu_custom_call" | custom-call | tf_op jit(solution)/shard_map/combine/pallas_call | solution.py:689
